TPU v7x, 32 devices: a whole 2x2x4 slice. The times are simulated.
32 devices in a mesh: dp: 2 (over x), row: 4 (over z), col: 4 (over y, core).
Axes of the slice: x: 2, y: 2, z: 4, core: 2. Of those that a mesh axis runs over, the one named last changes fastest.
Arguments:
- x_in: bfloat16 [4, 1024, 2560], P('dp', None, ('row', 'col')), parts along dimension 0
- ln_gain: bfloat16 [2, 2560], P(None, ('row', 'col'))
- w_in: bfloat16 [2, 2560, 23040], P(None, 'row', 'col')
- w_kv: bfloat16 [2, 2560, 160], P(None, 'row', 'col')
- w_out: bfloat16 [2, 12800, 2560], P(None, 'col', 'row')
Outputs:
- output 1: bfloat16 [4, 1024, 2560], P('dp', None, ('row', 'col')), parts along dimension 0
- output 2: bfloat16 [2, 2, 4, 1024, 80], P(None, None, 'dp', ('row', 'col')), parts along dimension 2
There are 2 independent parts. A program takes and returns all parts, laid end to end along the dimension named above; an argument that names none is the same for every part.
All inputs are finite; a program needn't handle non-finite values.
Results may differ from a plain program's by a relative error of at most 0.015362.
Values are sent between devices in bfloat16 or wider.
A program may use at most 1 GiB of HBM per device.

v0:
```python
import jax
import jax.numpy as jnp
from jax import lax
from jax.sharding import PartitionSpec as P

LN_EPS = 1e-6


def rope_tables(positions, head_dim):
    half_dim = head_dim // 2
    inv_freq = 1.0 / (10000.0 ** (jnp.arange(half_dim, dtype=jnp.float32) * 2.0 / head_dim))
    angles = positions.astype(jnp.float32)[:, None] * inv_freq[None, :]
    return jnp.cos(angles), jnp.sin(angles)


def apply_rope(values, cos_tab, sin_tab):
    half_dim = values.shape[-1] // 2
    lower_half = values[..., :half_dim]
    upper_half = values[..., half_dim:]
    return jnp.concatenate([lower_half * cos_tab - upper_half * sin_tab, upper_half * cos_tab + lower_half * sin_tab], axis=-1)


def solution(mesh):
    row_size = mesh.shape["row"]
    col_size = mesh.shape["col"]
    act_spec = P("dp", None, ("row", "col"))
    weight_spec = P(None, "row", "col")

    def device_fn(x_loc, gain_loc, w_in_loc, w_kv_loc, w_out_loc):
        n_layers = w_in_loc.shape[0]
        n_batch, seq_len, d_local = x_loc.shape
        d_model = d_local * row_size * col_size
        e_block = w_in_loc.shape[2]
        r_block = w_out_loc.shape[1]
        f_block = e_block - r_block
        q_block = r_block - f_block
        head_dim = w_kv_loc.shape[2] * col_size // 2
        heads_local = q_block // head_dim
        seq_local = seq_len // (row_size * col_size)
        shard_index = lax.axis_index("row") * col_size + lax.axis_index("col")
        positions = jnp.arange(seq_len)
        cos_tab, sin_tab = rope_tables(positions, head_dim)
        causal = positions[None, :] <= positions[:, None]
        hidden = x_loc
        kv_outs = []
        for layer_idx in range(n_layers):
            hidden_f32 = hidden.astype(jnp.float32)
            tok_sum = lax.psum(jnp.sum(hidden_f32, axis=-1, keepdims=True), ("row", "col"))
            centered = hidden_f32 - tok_sum / d_model
            sq_sum = lax.psum(jnp.sum(centered * centered, axis=-1, keepdims=True), ("row", "col"))
            normed = (centered * lax.rsqrt(sq_sum / d_model + LN_EPS) * gain_loc[layer_idx].astype(jnp.float32)).astype(jnp.bfloat16)
            normed_row = lax.all_gather(normed, "col", axis=2, tiled=True)
            part_main = jnp.einsum("bsd,de->bse", normed_row, w_in_loc[layer_idx], preferred_element_type=jnp.float32).astype(jnp.bfloat16)
            part_kv = jnp.einsum("bsd,de->bse", normed_row, w_kv_loc[layer_idx], preferred_element_type=jnp.float32).astype(jnp.bfloat16)
            main_proj, kv_piece = lax.psum((part_main, part_kv), "row")
            kv_proj = lax.all_gather(kv_piece, "col", axis=2, tiled=True)
            query = main_proj[..., :q_block].reshape(n_batch, seq_len, heads_local, head_dim)
            gate_val = main_proj[..., q_block:q_block + f_block]
            up_val = main_proj[..., q_block + f_block:]
            q_rot = (apply_rope(query.astype(jnp.float32), cos_tab[:, None, :], sin_tab[:, None, :]) * head_dim ** -0.5).astype(jnp.bfloat16)
            k_rot = apply_rope(kv_proj[..., :head_dim].astype(jnp.float32), cos_tab, sin_tab).astype(jnp.bfloat16)
            v_val = kv_proj[..., head_dim:]
            scores = jnp.einsum("crie,cle->cirl", q_rot, k_rot, preferred_element_type=jnp.float32)
            scores = jnp.where(causal, scores, -1e30)
            attn_prob = jax.nn.softmax(scores, axis=-1).astype(jnp.bfloat16)
            attn_out = jnp.einsum("cirl,cle->crie", attn_prob, v_val, preferred_element_type=jnp.float32).astype(jnp.bfloat16).reshape(n_batch, seq_len, q_block)
            mlp_out = (jax.nn.silu(gate_val.astype(jnp.float32)) * up_val.astype(jnp.float32)).astype(jnp.bfloat16)
            joined = jnp.concatenate([attn_out, mlp_out], axis=2)
            part_out = jnp.einsum("bsr,rd->bsd", joined, w_out_loc[layer_idx], preferred_element_type=jnp.float32).astype(jnp.bfloat16)
            update = lax.psum_scatter(part_out, "col", scatter_dimension=2, tiled=True)
            hidden = hidden + update
            kv_outs.append(lax.dynamic_slice_in_dim(jnp.stack([k_rot, v_val]), shard_index * seq_local, seq_local, axis=2))
        return hidden, jnp.stack(kv_outs)

    return jax.shard_map(device_fn, mesh=mesh, in_specs=(act_spec, P(None, ("row", "col")), weight_spec, weight_spec, P(None, "col", "row")), out_specs=(act_spec, P(None, None, "dp", ("row", "col"), None)), check_vma=False)
```

profile of v0, /device:TPU:8, one launch (start us, length us, event | category | flops | bytes accessed | tf_op | source)
XLA Modules:
  0.0 2113.9 jit_solution(7362915687584450758)
XLA Ops:
  9.7 25.9 %psum.56 = f32[2,1024,1]{1,0,2:T(2,128)S(1)} all-reduce(f32[2,1024,1]{1,0,2:T(2,128)S(1)} %bitcast.139), channel_id=1, replica_groups=mesh['dp'=2,'row'=4,'col'=4] {'row','col'}, use_global_device_ids=true, to_apply=%region_1.0 | all-reduce | flops 2048 | bytes 16384 | tf_op jit(solution)/shard_map/psum | solution.py:48
  36.9 30.0 %psum.57 = f32[2,1024,1]{1,0,2:T(2,128)S(1)} all-reduce(f32[2,1024,1]{1,0,2:T(2,128)S(1)} %bitcast.137), channel_id=1, replica_groups=mesh['dp'=2,'row'=4,'col'=4] {'row','col'}, use_global_device_ids=true, to_apply=%region_3.0 | all-reduce | flops 2048 | bytes 16384 | tf_op jit(solution)/shard_map/psum | solution.py:50
  69.2 30.6 %all-gather.3.cloned.1.call-done = bf16[2,1024,640]{1,2,0:T(8,128)(2,1)} async-done(((bf16[2,1024,160]{1,2,0:T(8,128)(2,1)}), bf16[2,1024,640]{1,2,0:T(8,128)(2,1)}) %all-gather.3.cloned.1.call-update) | async-done | bytes 2621456 | tf_op jit(solution)/shard_map/all_gather | solution.py:52
  99.7 3.0 convolution_convert_fusion.3
  102.7 25.6 %convolution_convert_fusion.1 = bf16[2,1024,5760]{2,1,0:T(8,128)(2,1)} fusion(bf16[2,1024,640]{1,2,0:T(8,128)(2,1)} %all-gather.3.cloned.1.call-done, bf16[2,640,5760]{2,1,0:T(8,128)(2,1)} %param.7), kind=kOutput, calls=%fused_computation.31 | convolution fusion | flops 15111290880 | bytes 33587200 | tf_op jit(solution)/shard_map/bsd,de->bse/dot_general | solution.py:53
  129.4 782.5 %all-reduce.7.cloned.1.call-done = (bf16[2,1024,5760]{2,1,0:T(8,128)(2,1)}, bf16[2,1024,40]{1,2,0:T(8,128)(2,1)}) async-done(((bf16[2,1024,5760]{2,1,0:T(8,128)(2,1)}, bf16[2,1024,40]{1,2,0:T(8,128)(2,1)}), (bf16[2,1024,5760]{2,1,0:T(8,128)(2,1)}, bf16[2,1024,40]{1,2,0:T(8,128)(2,1)})) %all-reduce.7.cloned.1.call-update) | async-done | bytes 23756816 | tf_op jit(solution)/shard_map/psum | solution.py:55
  911.9 4.4 slice_convert_fusion.1
  916.3 15.0 fusion.19
  931.3 8.2 all_gather.13
  940.3 5.9 copy.17
  946.3 6.3 multiply_subtract_fusion.1
  952.6 29.4 %fusion.114 = (f32[2,8,1024]{2,1,0:T(8,128)S(1)}, f32[2,8,1024,1024]{2,3,1,0:T(8,128)}) fusion(pred[1024,1024]{0,1:T(8,128)(4,1)S(1)} %iota_compare_fusion, bf16[2,1024,40]{1,2,0:T(8,128)(2,1)S(1)} %get-tuple-element.15, bf16[2,1024,40]{1,2,0:T(8,128)(2,1)S(1)} %get-tuple-element.14, f32[2,1024,8,40]{1,3,2,0:T(8,128)} %get-tuple-element.11, ...), kind=kOutput, calls=%fused_computation.138 | convolution fusion | flops 2739274752 | bytes 73793536 | tf_op jit(solution)/shard_map/sub | solution.py:65
  982.0 24.1 %fusion.53 = bf16[2,80,8,1024]{3,1,2,0:T(8,128)(2,1)} fusion(f32[2,8,1024,1024]{2,3,1,0:T(8,128)} %get-tuple-element.25, f32[2,8,1024]{2,1,0:T(8,128)S(1)} %get-tuple-element.24, bf16[2,1024,160]{1,2,0:T(8,128)(2,1)S(1)} %all_gather.13), kind=kOutput, calls=%fused_computation.64 | convolution fusion | flops 2719219712 | bytes 70123520 | tf_op jit(solution)/shard_map/cirl,cle->crie/dot_general | solution.py:66
  1006.1 3.1 copy.19
  1009.2 14.2 fusion.47
  1023.5 34.5 %reduce-scatter.3.cloned.1.call-done = bf16[2,1024,160]{1,2,0:T(8,128)(2,1)} async-done(((bf16[2,1024,640]{1,2,0:T(8,128)(2,1)}), bf16[2,1024,160]{1,2,0:T(8,128)(2,1)}) %reduce-scatter.3.cloned.1.call-update) | async-done | bytes 655376 | tf_op jit(solution)/shard_map/reduce_scatter | solution.py:70
  1059.4 24.5 %psum.60 = f32[2,1024,1]{1,0,2:T(2,128)S(1)} all-reduce(f32[2,1024,1]{1,0,2:T(2,128)S(1)} %bitcast.136), channel_id=1, replica_groups=mesh['dp'=2,'row'=4,'col'=4] {'row','col'}, use_global_device_ids=true, to_apply=%region_10.11 | all-reduce | flops 2048 | bytes 16384 | tf_op jit(solution)/shard_map/psum | solution.py:48
  1084.1 30.0 %psum.61 = f32[2,1024,1]{1,0,2:T(2,128)S(1)} all-reduce(f32[2,1024,1]{1,0,2:T(2,128)S(1)} %bitcast.138), channel_id=1, replica_groups=mesh['dp'=2,'row'=4,'col'=4] {'row','col'}, use_global_device_ids=true, to_apply=%region_12.13 | all-reduce | flops 2048 | bytes 16384 | tf_op jit(solution)/shard_map/psum | solution.py:50
  1115.3 30.5 %all-gather.5.cloned.1.call-done = bf16[2,1024,640]{1,2,0:T(8,128)(2,1)} async-done(((bf16[2,1024,160]{1,2,0:T(8,128)(2,1)}), bf16[2,1024,640]{1,2,0:T(8,128)(2,1)}) %all-gather.5.cloned.1.call-update) | async-done | bytes 2621456 | tf_op jit(solution)/shard_map/all_gather | solution.py:52
  1145.8 2.9 convolution_convert_fusion.2
  1148.8 25.8 %convolution_convert_fusion = bf16[2,1024,5760]{2,1,0:T(8,128)(2,1)} fusion(bf16[2,1024,640]{1,2,0:T(8,128)(2,1)} %all-gather.5.cloned.1.call-done, bf16[2,640,5760]{2,1,0:T(8,128)(2,1)} %param.7), kind=kOutput, calls=%fused_computation.30 | convolution fusion | flops 15111290880 | bytes 33587200 | tf_op jit(solution)/shard_map/bsd,de->bse/dot_general | solution.py:53
  1174.7 783.5 %all-reduce.5.cloned.1.call-done = (bf16[2,1024,5760]{2,1,0:T(8,128)(2,1)}, bf16[2,1024,40]{1,2,0:T(8,128)(2,1)}) async-done(((bf16[2,1024,5760]{2,1,0:T(8,128)(2,1)}, bf16[2,1024,40]{1,2,0:T(8,128)(2,1)}), (bf16[2,1024,5760]{2,1,0:T(8,128)(2,1)}, bf16[2,1024,40]{1,2,0:T(8,128)(2,1)})) %all-reduce.5.cloned.1.call-update) | async-done | bytes 23756816 | tf_op jit(solution)/shard_map/psum | solution.py:55
  1958.2 4.4 slice_convert_fusion
  1962.6 15.0 fusion.18
  1977.6 8.0 all_gather.15
  1986.5 6.3 copy.21
  1992.8 6.3 multiply_subtract_fusion
  1999.1 29.4 %fusion.119 = (f32[2,8,1024]{2,1,0:T(8,128)S(1)}, f32[2,8,1024,1024]{2,3,1,0:T(8,128)}) fusion(pred[1024,1024]{0,1:T(8,128)(4,1)S(1)} %copy-done.8, bf16[2,1024,40]{1,2,0:T(8,128)(2,1)S(1)} %get-tuple-element.13, bf16[2,1024,40]{1,2,0:T(8,128)(2,1)S(1)} %get-tuple-element.12, f32[2,1024,8,40]{1,3,2,0:T(8,128)} %get-tuple-element.9, ...), kind=kOutput, calls=%fused_computation.139 | convolution fusion | flops 2739274752 | bytes 73793536 | tf_op jit(solution)/shard_map/sub | solution.py:65
  2028.5 24.1 %fusion.52 = bf16[2,80,8,1024]{3,1,2,0:T(8,128)(2,1)} fusion(f32[2,8,1024,1024]{2,3,1,0:T(8,128)} %get-tuple-element.27, f32[2,8,1024]{2,1,0:T(8,128)S(1)} %get-tuple-element.26, bf16[2,1024,160]{1,2,0:T(8,128)(2,1)S(1)} %all_gather.15), kind=kOutput, calls=%fused_computation.63 | convolution fusion | flops 2719219712 | bytes 70123520 | tf_op jit(solution)/shard_map/cirl,cle->crie/dot_general | solution.py:66
  2052.6 3.1 copy.23
  2055.8 14.4 fusion.42
  2072.1 32.7 %reduce-scatter.5.cloned.1.call-done = bf16[2,1024,160]{1,2,0:T(8,128)(2,1)} async-done(((bf16[2,1024,640]{1,2,0:T(8,128)(2,1)}), bf16[2,1024,160]{1,2,0:T(8,128)(2,1)}) %reduce-scatter.5.cloned.1.call-update) | async-done | bytes 655376 | tf_op jit(solution)/shard_map/reduce_scatter | solution.py:70
  (72 shorter events, 15.8 us)
Async XLA Ops:
  7.2 92.6 %all-gather.3.cloned.1.call-start = ((), (), s32[]{:S(2)}) async-start(), calls=%async_computation.2 | async-start | bytes 3276800 | tf_op jit(solution)/shard_map/all_gather | solution.py:52
  69.1 842.8 %all-reduce.7.cloned.1.call-start = ((), (), s32[]{:S(2)}) async-start(), calls=%async_computation.7 | async-start | bytes 47513600 | tf_op jit(solution)/shard_map/psum | solution.py:55
  128.3 929.7 %reduce-scatter.3.cloned.1.call-start = ((), (), s32[]{:S(2)}) async-start(), calls=%async_computation.3 | async-start | bytes 3276800 | tf_op jit(solution)/shard_map/reduce_scatter | solution.py:70
  128.7 823.9 %copy-start.7 = (pred[1024,1024]{0,1:T(8,128)(4,1)}, pred[1024,1024]{0,1:T(8,128)(4,1)S(1)}, u32[]{:S(2)}) copy-start(pred[1024,1024]{0,1:T(8,128)(4,1)S(1)} %iota_compare_fusion) | copy-start | bytes 3145732
  129.4 816.9 %copy-start.3 = (f32[1024,40]{0,1:T(8,128)}, f32[1024,40]{0,1:T(8,128)S(1)}, u32[]{:S(2)}) copy-start(f32[1024,40]{0,1:T(8,128)S(1)} %get-tuple-element.20) | copy-start | bytes 491524
  129.4 816.9 %copy-start.5 = (f32[1024,40]{0,1:T(8,128)}, f32[1024,40]{0,1:T(8,128)S(1)}, u32[]{:S(2)}) copy-start(f32[1024,40]{0,1:T(8,128)S(1)} %get-tuple-element.21) | copy-start | bytes 491524
  916.3 15.0 copy-start.14
  946.3 6.3 copy-start.9
  946.3 6.3 copy-start.11
  1009.2 48.8 %copy-start = (bf16[2,1024,160]{1,2,0:T(8,128)(2,1)S(1)}, bf16[2,1024,160]{1,2,0:T(8,128)(2,1)}, u32[]{:S(2)}) copy-start(bf16[2,1024,160]{1,2,0:T(8,128)(2,1)} %param.5) | copy-start | bytes 1966084
  1023.5 90.7 %copy-start.17 = (f32[1,160]{1,0:T(1,128)S(1)}, f32[1,160]{1,0:T(1,128)}, u32[]{:S(2)}) copy-start(f32[1,160]{1,0:T(1,128)} %get-tuple-element.22) | copy-start | bytes 1924
  1023.5 122.4 %copy-start.16 = (bf16[2,640,40]{1,2,0:T(8,128)(2,1)S(1)}, bf16[2,640,40]{1,2,0:T(8,128)(2,1)}, u32[]{:S(2)}) copy-start(bf16[2,640,40]{1,2,0:T(8,128)(2,1)} %param.8) | copy-start | bytes 307204
  1023.5 122.3 %all-gather.5.cloned.1.call-start = ((), (), s32[]{:S(2)}) async-start(), calls=%async_computation.4 | async-start | bytes 3276800 | tf_op jit(solution)/shard_map/all_gather | solution.py:52
  1059.4 115.2 %copy-start.1 = (bf16[2,1024,160]{1,2,0:T(8,128)(2,1)}, bf16[2,1024,160]{1,2,0:T(8,128)(2,1)S(1)}, u32[]{:S(2)}) copy-start(bf16[2,1024,160]{1,2,0:T(8,128)(2,1)S(1)} %get-tuple-element.7) | copy-start | bytes 1966084
  1115.2 842.9 %all-reduce.5.cloned.1.call-start = ((), (), s32[]{:S(2)}) async-start(), calls=%async_computation.6 | async-start | bytes 47513600 | tf_op jit(solution)/shard_map/psum | solution.py:55
  1174.6 930.1 %reduce-scatter.5.cloned.1.call-start = ((), (), s32[]{:S(2)}) async-start(), calls=%async_computation.5 | async-start | bytes 3276800 | tf_op jit(solution)/shard_map/reduce_scatter | solution.py:70
  1962.6 15.0 copy-start.15
  1962.6 23.8 %copy-start.4 = (f32[1024,40]{0,1:T(8,128)S(1)}, f32[1024,40]{0,1:T(8,128)}, u32[]{:S(2)}) copy-start(f32[1024,40]{0,1:T(8,128)} %copy-done.3) | copy-start | bytes 491524
  1962.6 23.8 %copy-start.6 = (f32[1024,40]{0,1:T(8,128)S(1)}, f32[1024,40]{0,1:T(8,128)}, u32[]{:S(2)}) copy-start(f32[1024,40]{0,1:T(8,128)} %copy-done.5) | copy-start | bytes 491524
  1986.5 12.6 copy-start.12
  1986.5 12.6 copy-start.13
  1992.8 6.3 copy-start.8
  2055.7 14.5 copy-start.10
  2055.8 49.0 %copy-start.2 = (bf16[2,1024,160]{1,2,0:T(8,128)(2,1)S(1)}, bf16[2,1024,160]{1,2,0:T(8,128)(2,1)}, u32[]{:S(2)}) copy-start(bf16[2,1024,160]{1,2,0:T(8,128)(2,1)} %copy-done.1) | copy-start | bytes 1966084
Sparse Core Ops, SparseCore 0:
  69.2 30.4 all-gather.2
  128.5 783.3 all-reduce.6
  1023.6 34.3 reduce-scatter.2
  1115.4 30.4 all-gather.4
  1174.8 783.3 all-reduce.4
  2070.3 34.3 reduce-scatter.4
where the time goes:
time: 2120 us; the launch traced here: 2110 us
  waiting for transfers between devices  1690 us (80%)
  matrix products  193 us (9%)
  blocking collectives  127 us (6%)
  other arithmetic  66.6 us (3%)
    psum x2, waiting for transfers between devices, device_fn(): main_proj, kv_piece = lax.psum((part_main, part_kv), 'row')  1570 us
    reduce_scatter x2, waiting for transfers between devices, device_fn(): update = lax.psum_scatter(part_out, 'col', scatter_dimension=2, tiled=True)  67.1 us
    all_gather x2, waiting for transfers between devices, device_fn(): normed_row = lax.all_gather(normed, 'col', axis=2, tiled=True)  61.1 us
    psum x2, blocking collectives, device_fn(): lax.psum(jnp.sum(centered * centered, axis=-1, keepdims=True), ('row', 'c...  60 us
    sub x2, matrix products, device_fn(): attn_prob = jax.nn.softmax(scores, axis=-1).astype(jnp.bfloat16)  58.8 us
    dot_general x2, matrix products, device_fn(): jnp.einsum('bsd,de->bse', normed_row, w_in_loc[layer_idx], preferred_elem...  51.5 us
    psum x2, blocking collectives, device_fn(): lax.psum(jnp.sum(hidden_f32, axis=-1, keepdims=True), ('row', 'col'))  50.4 us
    dot_general x2, matrix products, device_fn(): jnp.einsum('cirl,cle->crie', attn_prob, v_val, preferred_element_type=jnp...  48.1 us
  transfers between devices with their start and end apart: 6, of which 6 were waited for; matrix products, arithmetic and copies ran while one was open for 0% of the time, Pallas kernels for 0%

commit v1 on v0

v1 whole, which is shorter than its diff:
```python
import functools

import jax
import jax.numpy as jnp
from jax import lax
from jax.experimental import pallas as pl
from jax.experimental.pallas import tpu as pltpu
from jax.sharding import PartitionSpec as P

BF = jnp.bfloat16
F32 = jnp.float32
MESH_ID = pl.DeviceIdType.MESH
LN_EPS = 1e-6

D = 2560
SH = 160
RW = 640
FB = 640
HD = 80
HALF = HD // 2
SEQ = 1024
T = 2 * SEQ
CW = 512
NT = T // CW
NE = 512 // CW
NC = NE + NT
GP = 4
GR = RW // GP
QB = 256


def rope_tables():
    inv_freq = 1.0 / (10000.0 ** (jnp.arange(HALF, dtype=F32) * 2.0 / HD))
    angles = inv_freq[:, None] * jnp.arange(SEQ).astype(F32)[None, :]
    return jnp.stack([jnp.cos(angles), jnp.sin(angles)])


def dot_ta(a, b):
    return lax.dot_general(a, b, (((0,), (0,)), ((), ())), preferred_element_type=F32)


def kernel(xin, wq, w_in, w_out, cs, yT, kvo, XA, GU, WQ, WKV, WO, GB, MT, QT, KT, VT, XO, RC, RY, RU, RD, SC, SY, SZ,
           zsu, zsd, ysn, csn, zrc, yrc, crc, rcs, rcr, rys, ryr, rzu, rzd, rsu, rsd, ws, wr, xs, xr, own):
    x = lax.axis_index("dp")
    z = lax.axis_index("row")
    c = lax.axis_index("col")
    y, k = c // 2, lax.rem(c, 2)
    me = 4 * z + c
    up = (x, jnp.minimum(z + 1, 3), c)
    down = (x, jnp.maximum(z - 1, 0), c)
    ypeer = (x, z, lax.rem(c + 2, 4))
    cpeer = (x, z, c + 1 - 2 * k)
    xpeer = (1 - x, z, c)
    zpeer = [(x, lax.rem(z + h, 4), c) for h in (1, 2, 3)]

    def rcopy(src, dst, ss, rs, dev):
        return pltpu.make_async_remote_copy(src_ref=src, dst_ref=dst, send_sem=ss, recv_sem=rs, device_id=dev, device_id_type=MESH_ID)

    def wait_for(ref, sem):
        pltpu.make_async_copy(ref, ref, sem).wait()

    def rows(s):
        return pl.ds(pl.multiple_of(s * SH, SH), SH)

    def loop(n, body):
        def step(i, carry):
            body(i)
            return carry
        lax.fori_loop(0, n, step, 0)

    barrier = pltpu.get_barrier_semaphore()
    for dev in zpeer + [ypeer, cpeer, xpeer]:
        pl.semaphore_signal(barrier, inc=1, device_id=dev, device_id_type=MESH_ID)
    pl.semaphore_wait(barrier, 6)

    def act(ch, s):
        return XA.at[ch, rows(s)]

    def ext(ch, s):
        i = 16 * ch + s
        return MT.at[i // 5, rows(lax.rem(i, 5))]

    def gather_own(src, buf, ch, o):
        q = ch + o
        dst = buf(ch, me)

        @pl.when(z < 3)
        def _():
            rcopy(src, dst, zsu.at[q], zrc.at[q, 0, 0], up).start()

        @pl.when(z > 0)
        def _():
            rcopy(src, dst, zsd.at[q], zrc.at[q, 1, 0], down).start()

        rcopy(src, dst, ysn.at[q], yrc.at[q], ypeer).start()
        rcopy(src, dst, csn.at[q], crc.at[q], cpeer).start()

    def gather_hop(buf, ch, o, hop):
        q = ch + o

        @pl.when(z - hop >= 0)
        def _():
            ref = buf(ch, jnp.maximum(me - 4 * hop, 0))
            wait_for(ref, zrc.at[q, 0, hop - 1])
            if hop < 3:
                @pl.when(z < 3)
                def _():
                    rcopy(ref, ref, zsu.at[q], zrc.at[q, 0, hop], up).start()
            rcopy(ref, ref, ysn.at[q], yrc.at[q], ypeer).start()
            rcopy(ref, ref, csn.at[q], crc.at[q], cpeer).start()

        @pl.when(z + hop <= 3)
        def _():
            ref = buf(ch, jnp.minimum(me + 4 * hop, 15))
            wait_for(ref, zrc.at[q, 1, hop - 1])
            if hop < 3:
                @pl.when(z > 0)
                def _():
                    rcopy(ref, ref, zsd.at[q], zrc.at[q, 1, hop], down).start()
            rcopy(ref, ref, ysn.at[q], yrc.at[q], ypeer).start()
            rcopy(ref, ref, csn.at[q], crc.at[q], cpeer).start()

    def gather_cross(buf, ch, o):
        q = ch + o
        wait_for(XA.at[0, pl.ds(0, 4 * SH)], yrc.at[q])
        for zz in range(4):
            ref = buf(ch, 4 * zz + lax.rem(c + 2, 4))
            rcopy(ref, ref, csn.at[q], crc.at[q], cpeer).start()

    def gather_end(buf, ch, o):
        q = ch + o
        wait_for(XA.at[0, pl.ds(0, 8 * SH)], crc.at[q])
        for zz in range(3):
            @pl.when(z == zz)
            def _():
                wait_for(XA.at[0, pl.ds(0, (zz + 1) * SH)], zsu.at[q])

            @pl.when(z == 3 - zz)
            def _():
                wait_for(XA.at[0, pl.ds(0, (zz + 1) * SH)], zsd.at[q])
        wait_for(XA.at[0, pl.ds(0, 4 * SH)], ysn.at[q])
        wait_for(XA.at[0, pl.ds(0, 8 * SH)], csn.at[q])

    NPC = GP + 3

    def lane(zz):
        return pl.ds(pl.multiple_of(zz * RW, 128), RW)

    def w_ref(l, p, zz, half):
        if p == 0:
            return WQ.at[l, pl.ds(pl.multiple_of(80 * half, 16), 80), lane(zz)]
        if p <= GP:
            return GU.at[l, half, pl.ds(pl.multiple_of(zz * RW + GR * (p - 1), 16), GR), :]
        if p == GP + 1:
            return WO.at[l, pl.ds(pl.multiple_of(400 * half, 16), 160), lane(zz)]
        return WO.at[l, pl.ds(pl.multiple_of(160 + 400 * half, 16), 240), lane(zz)]

    def w_src(l, p, t):
        if p == 0:
            return wq.at[l, pl.ds(pl.multiple_of(SH * t + 80 * x, 16), 80), :]
        if p <= GP:
            return w_in.at[l, pl.ds(GR * (p - 1), GR), pl.ds(pl.multiple_of(RW + D * x + FB * t, 128), FB)]
        if p == GP + 1:
            row = jnp.where(x == 0, SH * t, RW + FB * t + 240)
            return w_out.at[l, pl.ds(pl.multiple_of(row, 16), 160), :]
        return w_out.at[l, pl.ds(pl.multiple_of(RW + FB * t + 400 * x, 16), 240), :]

    def w_send(l, p):
        for h in (1, 2, 3):
            t = lax.rem(z + h, 4)
            rcopy(w_src(l, p, t), w_ref(l, p, z, x), ws.at[l, p], wr.at[l, p, h - 1], zpeer[h - 1]).start()

    def w_forward(l, p):
        for h in (1, 2, 3):
            ref = w_ref(l, p, lax.rem(z - h + 4, 4), x)
            wait_for(ref, wr.at[l, p, h - 1])
            rcopy(ref, ref, xs.at[l, p], xr.at[l, p], xpeer).start()

    def w_size(l, p):
        if p == 0:
            return WQ.at[l, pl.ds(0, 80), pl.ds(0, 3 * RW)]
        if p <= GP:
            return GU.at[l, 0, pl.ds(0, 3 * GR), :]
        if p == GP + 1:
            return WO.at[l, pl.ds(0, 160), pl.ds(0, 3 * RW)]
        return WO.at[l, pl.ds(0, 240), pl.ds(0, 3 * RW)]

    def w_arrive(l, p):
        wait_for(w_size(l, p), xr.at[l, p])

    def w_own(l):
        return [
            pltpu.make_async_copy(wq.at[l, pl.ds(pl.multiple_of(SH * z, 16), SH), :], WQ.at[l, :, lane(z)], own.at[l, 0]),
            pltpu.make_async_copy(w_in.at[l, :, pl.ds(pl.multiple_of(RW + FB * z, 128), FB)], GU.at[l, 0, pl.ds(pl.multiple_of(z * RW, 16), RW), :], own.at[l, 1]),
            pltpu.make_async_copy(w_in.at[l, :, pl.ds(pl.multiple_of(RW + D + FB * z, 128), FB)], GU.at[l, 1, pl.ds(pl.multiple_of(z * RW, 16), RW), :], own.at[l, 2]),
            pltpu.make_async_copy(w_out.at[l, pl.ds(pl.multiple_of(SH * z, 16), SH), :], WO.at[l, pl.ds(0, SH), lane(z)], own.at[l, 3]),
            pltpu.make_async_copy(w_out.at[l, pl.ds(pl.multiple_of(RW + FB * z, 16), FB), :], WO.at[l, pl.ds(SH, FB), lane(z)], own.at[l, 4]),
        ]

    for ch in range(NE):
        gather_own(xin.at[ch], ext, ch, 0)
    for ch in range(NT):
        gather_own(xin.at[NE + ch], act, ch, NE)
    for ch in range(NE):
        ext(ch, me)[...] = xin[ch]

    def put_own(ch):
        XA[ch, rows(me)] = xin[NE + ch]
    loop(NT, put_own)
    w_send(0, 0)
    w_send(0, 1)
    for l in range(2):
        for cp in w_own(l):
            cp.start()
    for hop in (1, 2, 3):
        loop(NE, lambda ch: gather_hop(ext, ch, 0, hop))
    loop(NE, lambda ch: gather_cross(ext, ch, 0))

    def unpack():
        loop(NE, lambda ch: gather_end(ext, ch, 0))

        def shard(s):
            zz, cc = s // 4, lax.rem(s, 4)
            for b in range(5):
                lo = 128 * (b // 2)
                i = 16 * (lo // CW) + s
                blk = MT[i // 5, pl.ds(pl.multiple_of(lax.rem(i, 5) * SH + 80 * (b % 2), 16), 80), lo % CW:lo % CW + 128].astype(F32)
                for l in range(2):
                    WKV[l, pl.ds(pl.multiple_of(48 * cc, 16), 40), pl.ds(pl.multiple_of(zz * RW + 128 * b, 128), 128)] = blk[40 * l:40 * l + 40].astype(BF)
            i = 16 * (NE - 1) + s
            blk = MT[i // 5, rows(lax.rem(i, 5)), CW - 128:CW].astype(F32)
            for l in range(2):
                GB[l, rows(s), :] = jnp.broadcast_to(blk[:, l:l + 1], (SH, 128)).astype(BF)
        loop(16, shard)
        for l in range(2):
            for cc in range(4):
                WKV[l, 48 * cc + 40:48 * cc + 48, :] = jnp.zeros((8, D), BF)

    BR = 32

    def norm(l, n):
        def fold(v):
            return v.reshape(BR // 8, 8, CW).sum(0)

        def load(i):
            return XA[n, pl.ds(pl.multiple_of(i * BR, BR), BR), :].astype(F32)

        tot = lax.fori_loop(0, D // BR, lambda i, a: a + fold(load(i)), jnp.zeros((8, CW), F32), unroll=4)
        mean = jnp.sum(tot, axis=0, keepdims=True) / D

        def square(i, a):
            d = load(i) - mean
            return a + fold(d * d)
        var = jnp.sum(lax.fori_loop(0, D // BR, square, jnp.zeros((8, CW), F32), unroll=4), axis=0, keepdims=True) / D
        scale = lax.rsqrt(var + LN_EPS)

        def put(i, a):
            g = jnp.concatenate([GB[l, pl.ds(pl.multiple_of(i * BR, BR), BR), :].astype(F32)] * (CW // 128), axis=1)
            XA[n, pl.ds(pl.multiple_of(i * BR, BR), BR), :] = ((load(i) - mean) * scale * g).astype(BF)
            return a
        lax.fori_loop(0, D // BR, put, 0, unroll=4)

    def tok(n):
        return pl.ds(pl.multiple_of(n * CW, 128), CW)

    def qkv(l, n):
        pos = pl.ds(pl.multiple_of(lax.rem(n * CW, SEQ), 128), CW)
        co, si = cs[0, :, pos], cs[1, :, pos]
        h = XA[n]
        kv = jnp.dot(WKV[l], h, preferred_element_type=F32).astype(BF).astype(F32)

        def rot(lo, hi):
            return jnp.concatenate([lo * co - hi * si, hi * co + lo * si], axis=0)
        KT[:, tok(n)] = rot(kv[0:40], kv[48:88]).astype(BF)
        VT[:, tok(n)] = jnp.concatenate([kv[96:136], kv[144:184]], axis=0).astype(BF)
        qq = jnp.dot(WQ[l], h, preferred_element_type=F32).astype(BF).astype(F32)
        for hd in range(2):
            QT[HD * hd:HD * hd + HD, tok(n)] = (rot(qq[HD * hd:HD * hd + HALF], qq[HD * hd + HALF:HD * hd + HD]) * HD ** -0.5).astype(BF)

    def attention():
        def body(bh):
            b, hd = bh // 2, lax.rem(bh, 2)
            hr = pl.ds(pl.multiple_of(hd * HD, 16), HD)
            for i in range(SEQ // QB):
                nk = QB * (i + 1)
                ks = pl.ds(pl.multiple_of(b * SEQ, 128), nk)
                qs = pl.ds(pl.multiple_of(b * SEQ + QB * i, 128), QB)
                s = dot_ta(KT[:, ks], QT[hr, qs])
                keep = lax.broadcasted_iota(jnp.int32, (QB, QB), 0) <= lax.broadcasted_iota(jnp.int32, (QB, QB), 1)
                last = jnp.where(keep, s[nk - QB:], -1e30)
                s = jnp.concatenate([s[:nk - QB], last], axis=0) if i else last
                e = jnp.exp(s - jnp.max(s, axis=0, keepdims=True))
                pr = (e * (1.0 / jnp.sum(e, axis=0, keepdims=True))).astype(BF)
                MT[b * (SEQ // CW) + QB * i // CW, hr, QB * i % CW:QB * i % CW + QB] = jnp.dot(VT[:, ks], pr, preferred_element_type=F32).astype(BF)
        loop(4, body)

    def gate_up(l, n):
        h = XA[n]
        g = dot_ta(GU[l, 0], h).astype(BF).astype(F32)
        u = dot_ta(GU[l, 1], h).astype(BF).astype(F32)
        MT[n, SH:SH + FB, :] = (g * lax.logistic(g) * u).astype(BF)

    def f(ref_value):
        return ref_value.astype(F32)

    def red_a(l, n):
        m = MT[n]
        slot = lax.rem(n, 2)

        @pl.when(n >= 2)
        def _():
            wait_for(RC.at[0], rcs.at[n - 2])

        def blk(zz):
            XA[n, pl.ds(pl.multiple_of(zz * RW, RW), RW), :] = dot_ta(WO[l, :, lane(zz)], m).astype(BF)
            for yy in range(2):
                SC[slot, 2 * zz + yy] = XA[n, rows(4 * zz + 2 * yy + 1 - k)]
                rcopy(SC.at[slot, 2 * zz + yy], RC.at[n, 2 * zz + yy], rcs.at[n], rcr.at[n], cpeer).start()
        loop(4, blk)

    def red_b(n):
        slot = lax.rem(n, 2)
        wait_for(RC.at[n], rcr.at[n])

        @pl.when(n >= 2)
        def _():
            wait_for(RY.at[0], rys.at[n - 2])

        for zz in (3, 0, 2, 1):
            SY[slot, zz] = (f(XA[n, rows(4 * zz + 2 * (1 - y) + k)]) + f(RC[n, 2 * zz + 1 - y])).astype(BF)
            rcopy(SY.at[slot, zz], RY.at[n, zz], rys.at[n], ryr.at[n], ypeer).start()

    def red_c(n):
        wait_for(RY.at[n], ryr.at[n])

        def part(zz):
            return f(XA[n, rows(4 * zz + c)]) + f(RC[n, 2 * zz + y]) + f(RY[n, zz])

        for zz in (3, 0, 2, 1):
            SZ[n, zz] = part(zz).astype(BF)

        @pl.when(z == 0)
        def _():
            for zz in (3, 2, 1):
                send_up(n, zz)

        @pl.when(z == 3)
        def _():
            for zz in (0, 1, 2):
                send_down(n, zz)

    def send_up(n, zz):
        rcopy(SZ.at[n, zz], RU.at[n, zz - 1], rsu.at[n], rzu.at[n, zz - 1], up).start()

    def send_down(n, zz):
        rcopy(SZ.at[n, zz], RD.at[n, zz], rsd.at[n], rzd.at[n, zz], down).start()

    def relay_up(n, zz):
        wait_for(RU.at[n, zz - 1], rzu.at[n, zz - 1])
        SZ[n, zz] = (f(SZ[n, zz]) + f(RU[n, zz - 1])).astype(BF)
        send_up(n, zz)

    def relay_down(n, zz):
        wait_for(RD.at[n, zz], rzd.at[n, zz])
        SZ[n, zz] = (f(SZ[n, zz]) + f(RD[n, zz])).astype(BF)
        send_down(n, zz)

    def red_d(n):
        @pl.when(z == 1)
        def _():
            for zz in (3, 2):
                relay_up(n, zz)

        @pl.when(z == 2)
        def _():
            for zz in (0, 1):
                relay_down(n, zz)

    def red_e(n):
        @pl.when(z == 2)
        def _():
            relay_up(n, 3)

        @pl.when(z == 1)
        def _():
            relay_down(n, 0)

    def red_f(l, n):
        s = rows(me)

        def finish(u):
            u = u.astype(BF)

            @pl.when(l == 0)
            def _():
                out = (f(xin[NE + n]) + f(u)).astype(BF)
                XO[n] = out
                XA[n, s] = out

            @pl.when(l == 1)
            def _():
                yT[n] = (f(XO[n]) + f(u)).astype(BF)

        @pl.when(z == 0)
        def _():
            wait_for(RD.at[n, 0], rzd.at[n, 0])
            finish(f(SZ[n, 0]) + f(RD[n, 0]))

        @pl.when(z == 3)
        def _():
            wait_for(RU.at[n, 2], rzu.at[n, 2])
            finish(f(SZ[n, 3]) + f(RU[n, 2]))

        for zz in (1, 2):
            @pl.when(z == zz)
            def _():
                wait_for(RU.at[n, zz - 1], rzu.at[n, zz - 1])
                wait_for(RD.at[n, zz], rzd.at[n, zz])
                finish(f(SZ[n, zz]) + f(RU[n, zz - 1]) + f(RD[n, zz]))

        @pl.when(n >= NT - 2)
        def _():
            wait_for(RC.at[0], rcs.at[n])
            wait_for(RY.at[0], rys.at[n])

        for zz in range(3):
            @pl.when(z == zz)
            def _():
                wait_for(RU.at[n, pl.ds(0, 3 - zz)], rsu.at[n])

            @pl.when(z == 3 - zz)
            def _():
                wait_for(RD.at[n, pl.ds(0, 3 - zz)], rsd.at[n])

        @pl.when(l == 0)
        def _():
            gather_own(XO.at[n], act, n, NE)

    shard = me

    def layer(l):
        for hop in (1, 2, 3):
            loop(NT, lambda n: gather_hop(act, n, NE, hop))
        loop(NT, lambda n: gather_cross(act, n, NE))

        for p in range(2, NPC):
            w_send(l, p)

        @pl.when(l == 0)
        def _():
            unpack()
        w_forward(l, 0)
        for i in range(5):
            wait_own(l, i)

        def first(n):
            gather_end(act, n, NE)
            norm(l, n)
            @pl.when(n == 0)
            def _():
                w_arrive(l, 0)
            qkv(l, n)
        loop(NT, first)
        w_forward(l, 1)
        w_forward(l, 2)
        attention()
        for b in range(2):
            off = pl.ds(pl.multiple_of(b * SEQ + 128 * (shard // 2), 128), 128)
            kvo[l, 0, b] = KT[:, off]
            kvo[l, 1, b] = VT[:, off]
        for p in range(3, GP + 1):
            w_forward(l, p)
        for p in range(1, GP + 1):
            w_arrive(l, p)
        loop(NT, lambda n: gate_up(l, n))
        for p in (GP + 1, GP + 2):
            w_forward(l, p)
        for p in (GP + 1, GP + 2):
            w_arrive(l, p)

        @pl.when(l == 0)
        def _():
            for p in range(2):
                w_send(1, p)

        def step(i):
            @pl.when(i < NT)
            def _():
                red_a(l, i)
            for lag, stage in ((1, red_b), (2, red_c), (3, red_d), (4, red_e), (5, functools.partial(red_f, l))):
                @pl.when((i >= lag) & (i < NT + lag))
                def _():
                    stage(i - lag)
        loop(NT + 5, step)

    def wait_own(l, i):
        ref = [WQ.at[0, :, pl.ds(0, RW)], GU.at[0, 0, pl.ds(0, RW)], GU.at[0, 0, pl.ds(0, RW)], WO.at[0, pl.ds(0, SH), pl.ds(0, RW)], WO.at[0, pl.ds(0, FB), pl.ds(0, RW)]][i]
        wait_for(ref, own.at[l, i])

    loop(2, layer)

    for l in range(2):
        for p in range(NPC):
            wait_for(w_size(l, p), ws.at[l, p])
            wait_for(w_size(l, p), xs.at[l, p])


def solution(mesh):
    act_spec = P("dp", None, ("row", "col"))
    weight_spec = P(None, "row", "col")

    def device_fn(x_loc, gain_loc, w_in_loc, w_kv_loc, w_out_loc):
        me = lax.axis_index("row") * 4 + lax.axis_index("col")
        xt = x_loc.reshape(T, SH).T
        kv = jnp.transpose(w_kv_loc, (0, 2, 1)).reshape(HD, 5, 128)
        kv = jnp.concatenate([kv, jnp.zeros((HD, 1, 128), BF)], axis=1).reshape(HD, 3, 2, 128)
        kv = jnp.transpose(kv, (2, 0, 1, 3)).reshape(SH, 384)
        gain = jnp.pad(gain_loc.T, ((0, 0), (0, 126)))
        xin = jnp.concatenate([kv, gain, xt], axis=1)
        xin = jnp.transpose(xin.reshape(SH, NC, CW), (1, 0, 2))
        wq = jnp.transpose(w_in_loc[:, :, :RW], (0, 2, 1))
        NPC = GP + 3
        dma = pltpu.SemaphoreType.DMA
        hbm = pl.BlockSpec(memory_space=pl.ANY)
        vmem = pl.BlockSpec(memory_space=pltpu.VMEM)
        y_t, kvo = pl.pallas_call(
            kernel,
            out_shape=(jax.ShapeDtypeStruct((NT, SH, CW), BF), jax.ShapeDtypeStruct((2, 2, 2, HD, 128), BF)),
            in_specs=[vmem, hbm, hbm, hbm, vmem],
            out_specs=(vmem, vmem),
            scratch_shapes=[
                pltpu.VMEM((NT, D, CW), BF),
                pltpu.VMEM((2, 2, D, FB), BF),
                pltpu.VMEM((2, SH, D), BF),
                pltpu.VMEM((2, 192, D), BF),
                pltpu.VMEM((2, SH + FB, D), BF),
                pltpu.VMEM((2, D, 128), BF),
                pltpu.VMEM((NT, SH + FB, CW), BF),
                pltpu.VMEM((SH, T), BF),
                pltpu.VMEM((HD, T), BF),
                pltpu.VMEM((HD, T), BF),
                pltpu.VMEM((NT, SH, CW), BF),
                pltpu.VMEM((NT, 8, SH, CW), BF),
                pltpu.VMEM((NT, 4, SH, CW), BF),
                pltpu.VMEM((NT, 3, SH, CW), BF),
                pltpu.VMEM((NT, 3, SH, CW), BF),
                pltpu.VMEM((2, 8, SH, CW), BF),
                pltpu.VMEM((2, 4, SH, CW), BF),
                pltpu.VMEM((NT, 4, SH, CW), BF),
                dma((NC,)), dma((NC,)), dma((NC,)), dma((NC,)),
                dma((NC, 2, 3)), dma((NC,)), dma((NC,)),
                dma((NT,)), dma((NT,)), dma((NT,)), dma((NT,)),
                dma((NT, 3)), dma((NT, 3)), dma((NT,)), dma((NT,)),
                dma((2, NPC)), dma((2, NPC, 3)), dma((2, NPC)), dma((2, NPC)),
                dma((2, 5)),
            ],
            compiler_params=pltpu.CompilerParams(collective_id=0, has_side_effects=True, vmem_limit_bytes=67043328),
        )(xin, wq, w_in_loc, w_out_loc, rope_tables())
        y = jnp.transpose(y_t, (0, 2, 1)).reshape(2, SEQ, SH)
        kv_out = lax.dynamic_slice_in_dim(kvo, 64 * lax.rem(me, 2), 64, axis=4)
        return y, jnp.transpose(kv_out, (0, 1, 2, 4, 3))

    return jax.shard_map(device_fn, mesh=mesh, in_specs=(act_spec, P(None, ("row", "col")), weight_spec, weight_spec, P(None, "col", "row")), out_specs=(act_spec, P(None, None, "dp", ("row", "col"), None)), check_vma=False)
```

time: 2120 us -> 565 us (0.27)
  waiting for transfers between devices: 1690 us -> 0 us
  Pallas kernels: 0 us -> 546 us
  matrix products: 193 us -> 0 us
  blocking collectives: 127 us -> 0 us
  other arithmetic: 66.6 us -> 1.48 us
    psum x2 -> x0, waiting for transfers between devices: 1570 us -> none  [device_fn(): main_proj, kv_piece = lax.psum((part_main, part_kv), 'row')]
    pallas_call x0 -> x1, Pallas kernels: none -> 546 us  [device_fn(): pl.pallas_call(kernel, out_shape=(jax.ShapeDtypeStruct((NT, SH, CW), BF),...]
    dot_general x8 -> x0, matrix products: 134 us -> none  [the longest x2 51.5 us: device_fn(): jnp.einsum('bsd,de->bse', normed_row, w_in_loc[layer_idx], preferred_elem...]
    psum x4 -> x0, blocking collectives: 110 us -> none  [the longest x2 60 us: device_fn(): lax.psum(jnp.sum(centered * centered, axis=-1, keepdims=True), ('row', 'c...]
    reduce_scatter x2 -> x0, waiting for transfers between devices: 67.1 us -> none  [device_fn(): update = lax.psum_scatter(part_out, 'col', scatter_dimension=2, tiled=True)]
    all_gather x2 -> x0, waiting for transfers between devices: 61.1 us -> none  [device_fn(): normed_row = lax.all_gather(normed, 'col', axis=2, tiled=True)]
    sub x2 -> x0, matrix products: 58.8 us -> none  [device_fn(): attn_prob = jax.nn.softmax(scores, axis=-1).astype(jnp.bfloat16)]
    convert_element_type x8 -> x1, other arithmetic: 43.3 us -> 0.01 us  [rope_tables(): angles = inv_freq[:, None] * jnp.arange(SEQ).astype(F32)[None, :]]
  transfers between devices with their start and end apart: 6 -> 0, of which waited for: 6 -> 0; matrix products, arithmetic and copies ran while one was open for 0% -> 0% of each run, Pallas kernels for 0% -> 0%
where the time goes in v1:
time: 565 us; the launch traced here: 558 us
  Pallas kernels  546 us (97%)
  local copies, waits for them, and re-layouts  10.1 us (2%)
    pallas_call x1, Pallas kernels, device_fn(): pl.pallas_call(kernel, out_shape=(jax.ShapeDtypeStruct((NT, SH, CW), BF),...  546 us

profile of v1, /device:TPU:8, one launch (start us, length us, event | category | flops | bytes accessed | tf_op | source)
XLA Modules:
  0.0 558.3 jit_solution(16047056946401056661)
XLA Ops:
  0.7 0.6 multiply_cosine_fusion
  1.3 0.7 pad_maximum_fusion.cs
  2.1 0.0 slice-start
  2.1 1.4 slice-done
  3.5 0.0 copy-start.1
  3.5 0.0 copy-start
  3.5 2.2 copy.19
  5.7 0.0 copy-start.2
  5.7 0.0 copy-done.1
  5.7 0.1 reshape.121
  5.9 0.1 copy.11
  6.0 0.0 copy-done
  6.0 0.3 copy-done.2
  6.3 0.1 copy.12
  6.5 0.1 fusion.3
  6.6 1.0 copy.26
  7.5 545.9 %shard_map.68 = (bf16[4,160,512]{2,1,0:T(8,128)(2,1)}, bf16[2,2,2,80,128]{4,3,2,1,0:T(8,128)(2,1)}) custom-call(bf16[5,160,512]{2,1,0:T(8,128)(2,1)} %bitcast.29, bf16[2,640,640]{2,1,0:T(8,128)(2,1)} %bitcast.27, bf16[2,640,5760]{2,1,0:T(8,128)(2,1)} %w_in.1, bf16[2,3200,640]{2,1,0:T(8,128)(2,1)} %w_out.1, f32[2,40,1024]{2,1,0:T(8,128)} %pad_maximum_fusion.cs), custom_call_target="tpu_custom_call" | custom-call | tf_op jit(solution)/shard_map/pallas_call | solution.py:526
  553.4 1.0 dynamic-slice_bitcast_fusion
  554.5 0.8 copy.18
  555.3 1.6 copy.16
  556.9 0.4 reshape.126
  557.3 1.0 copy.17
  (6 shorter events, 0.1 us)
Async XLA Ops:
  2.1 1.4 slice-start
  3.5 2.2 copy-start.1
  3.5 2.5 copy-start
  5.7 0.7 copy-start.2

commit v2 on v1

v2 whole, which is shorter than its diff:
```python
import functools

import jax
import jax.numpy as jnp
from jax import lax
from jax.experimental import pallas as pl
from jax.experimental.pallas import tpu as pltpu
from jax.sharding import PartitionSpec as P

BF = jnp.bfloat16
F32 = jnp.float32
MESH_ID = pl.DeviceIdType.MESH
LN_EPS = 1e-6

D = 2560
SH = 160
RW = 640
FB = 640
HD = 80
HALF = HD // 2
SEQ = 1024
T = 2 * SEQ
CW = 512
NT = T // CW
NE = 512 // CW
NC = NE + NT
GP = 8
GR = RW // GP
LANES = 128
HOPS = (1, 2, 3)
QB = 256
SCN, SYN = 4, 6
MR = 16
LAGS = (1, 3, 8, 12, 16)
PM = GR // MR
AG0 = 1
RQ = 0
RG = ((1, 11, 2),)
AG1 = (2,) * 10 + (0, 0)
UFW, EFW = 24, 5


def weight_plan():
    sent, when = 0, []
    for lo, hi, each in RG:
        for i in range(lo, hi):
            when += [i] * each
            sent += each
    units = [[] for _ in range(4 * NT + LAGS[-1])]
    events = [[] for _ in range(3 * NT)]
    late = list(range(1, GP + 1))
    ev = []
    for e in range(3 * NT):
        ev += [e] * AG1[e]
    for p in range(1, GP + 1):
        last = PM * p - 1
        if last < sent:
            if when[last] + UFW < len(units):
                units[when[last] + UFW].append(p)
                late.remove(p)
                continue
            e = max(0, when[last] + UFW - len(units))
        elif last < sent + len(ev):
            e = ev[last - sent] + EFW
        else:
            continue
        if e < 3 * NT:
            events[e].append(p)
            late.remove(p)
    return sent, units, events, late[0] if late else GP + 1


RS0, UNITS, EVENTS, LATE = weight_plan()


def rope_tables():
    inv_freq = 1.0 / (10000.0 ** (jnp.arange(HALF, dtype=F32) * 2.0 / HD))
    angles = inv_freq[:, None] * jnp.arange(SEQ).astype(F32)[None, :]
    return jnp.stack([jnp.cos(angles), jnp.sin(angles)])


def sub(start, size):
    return pl.ds(pl.multiple_of(start, 16), size)


def lan(start, size):
    return pl.ds(pl.multiple_of(start, LANES), size)


def dot_ta(a, b):
    return lax.dot_general(a, b, (((0,), (0,)), ((), ())), preferred_element_type=F32)


def kernel(xin, wq, w_in, w_out, cs, yT, kvo, XA, GU, WQ, WKV, WO, GB, MT, QT, KT, VT, XO, RC, RY, RU, RD, SC, SY, SZ,
           zsu, zsd, ysn, csn, zrc, yrc, crc, rcs, rcr, rys, ryr, rzu, rzd, rsz, ws, wr, xs, xr, own):
    x = lax.axis_index("dp")
    z = lax.axis_index("row")
    c = lax.axis_index("col")
    y, k = c // 2, lax.rem(c, 2)
    me = 4 * z + c
    up = (x, jnp.minimum(z + 1, 3), c)
    down = (x, jnp.maximum(z - 1, 0), c)
    ypeer = (x, z, lax.rem(c + 2, 4))
    cpeer = (x, z, c + 1 - 2 * k)
    xpeer = (1 - x, z, c)
    zpeer = [(x, lax.rem(z + h, 4), c) for h in HOPS]

    def rcopy(src, dst, ss, rs, dev):
        return pltpu.make_async_remote_copy(src_ref=src, dst_ref=dst, send_sem=ss, recv_sem=rs, device_id=dev, device_id_type=MESH_ID)

    def wait_for(ref, sem):
        pltpu.make_async_copy(ref, ref, sem).wait()

    def rows(s):
        return sub(s * SH, SH)

    def loop(n, body):
        def step(i, carry):
            body(i)
            return carry
        lax.fori_loop(0, n, step, 0)

    barrier = pltpu.get_barrier_semaphore()
    for dev in zpeer + [ypeer, cpeer, xpeer]:
        pl.semaphore_signal(barrier, inc=1, device_id=dev, device_id_type=MESH_ID)
    pl.semaphore_wait(barrier, 6)

    def act(ch, s):
        return XA.at[ch, rows(s)]

    def ext(ch, s):
        i = 16 * ch + s
        return MT.at[i // 5, rows(lax.rem(i, 5))]

    @jax.named_scope("gather_own")
    def gather_own(src, buf, ch, o):
        q = ch + o
        dst = buf(ch, me)

        @pl.when(z < 3)
        def _():
            rcopy(src, dst, zsu.at[q], zrc.at[q, 0, 0], up).start()

        @pl.when(z > 0)
        def _():
            rcopy(src, dst, zsd.at[q], zrc.at[q, 1, 0], down).start()

        rcopy(src, dst, ysn.at[q], yrc.at[q], ypeer).start()
        rcopy(src, dst, csn.at[q], crc.at[q], cpeer).start()

    @jax.named_scope("gather_hop")
    def gather_hop(buf, ch, o, hop):
        q = ch + o

        @pl.when(z - hop >= 0)
        def _():
            ref = buf(ch, jnp.maximum(me - 4 * hop, 0))
            wait_for(ref, zrc.at[q, 0, hop - 1])
            if hop < 3:
                @pl.when(z < 3)
                def _():
                    rcopy(ref, ref, zsu.at[q], zrc.at[q, 0, hop], up).start()
            rcopy(ref, ref, ysn.at[q], yrc.at[q], ypeer).start()
            rcopy(ref, ref, csn.at[q], crc.at[q], cpeer).start()

        @pl.when(z + hop <= 3)
        def _():
            ref = buf(ch, jnp.minimum(me + 4 * hop, 15))
            wait_for(ref, zrc.at[q, 1, hop - 1])
            if hop < 3:
                @pl.when(z > 0)
                def _():
                    rcopy(ref, ref, zsd.at[q], zrc.at[q, 1, hop], down).start()
            rcopy(ref, ref, ysn.at[q], yrc.at[q], ypeer).start()
            rcopy(ref, ref, csn.at[q], crc.at[q], cpeer).start()

    @jax.named_scope("gather_cross")
    def gather_cross(buf, ch, o):
        q = ch + o
        wait_for(XA.at[0, pl.ds(0, 4 * SH)], yrc.at[q])
        for zz in range(4):
            ref = buf(ch, 4 * zz + lax.rem(c + 2, 4))
            rcopy(ref, ref, csn.at[q], crc.at[q], cpeer).start()

    @jax.named_scope("gather_end")
    def gather_end(buf, ch, o):
        q = ch + o
        wait_for(XA.at[0, pl.ds(0, 8 * SH)], crc.at[q])
        for zz in range(3):
            @pl.when(z == zz)
            def _():
                wait_for(XA.at[0, pl.ds(0, (zz + 1) * SH)], zsu.at[q])

            @pl.when(z == 3 - zz)
            def _():
                wait_for(XA.at[0, pl.ds(0, (zz + 1) * SH)], zsd.at[q])
        wait_for(XA.at[0, pl.ds(0, 4 * SH)], ysn.at[q])
        wait_for(XA.at[0, pl.ds(0, 8 * SH)], csn.at[q])

    NPC = GP + 3

    def lane(zz):
        return lan(zz * RW, RW)

    PQ, PA, PB = 0, GP + 1, GP + 2

    def kind(p):
        return p if isinstance(p, int) and (p == PQ or p > GP) else 1

    def w_ref(l, p, zz, half):
        if kind(p) == PQ:
            return WQ.at[l, sub(80 * half, 80), lane(zz)]
        if kind(p) == PA:
            return WO.at[l, sub(400 * half, 160), lane(zz)]
        if kind(p) == PB:
            return WO.at[l, sub(160 + 400 * half, 240), lane(zz)]
        return GU.at[l, half, sub(zz * RW + GR * (p - 1), GR), :]

    def w_send(l, kind_, m, mr=MR):
        r = mr * m
        for h in HOPS:
            t = lax.rem(z + h, 4)
            if kind_ == "q":
                p, src = PQ, wq.at[l, sub(SH * t + 80 * x + r, mr), :]
                dst = WQ.at[l, sub(80 * x + r, mr), lane(z)]
            elif kind_ == "g":
                p, src = 1 + r // GR, w_in.at[l, sub(r, mr), lan(RW + D * x + FB * t, FB)]
                dst = GU.at[l, x, sub(z * RW + r, mr), :]
            elif kind_ == "a":
                p, src = PA, w_out.at[l, sub(jnp.where(x == 0, SH * t, RW + FB * t + 240) + r, mr), :]
                dst = WO.at[l, sub(400 * x + r, mr), lane(z)]
            else:
                p, src = PB, w_out.at[l, sub(RW + FB * t + 400 * x + r, mr), :]
                dst = WO.at[l, sub(160 + 400 * x + r, mr), lane(z)]
            rcopy(src, dst, ws.at[l, p], wr.at[l, p, h - 1], zpeer[h - 1]).start()

    def rest_send(l, m):
        whole = -(-m // PM)
        for v in range(m, whole * PM):
            w_send(l, "g", v)
        for v in range(whole, GP):
            w_send(l, "g", v, GR)

    NQ, NG, NA, NB = 80 // MR, RW // MR, 160 // MR, 240 // MR

    @jax.named_scope("w_forward")
    def w_forward(l, p):
        for h in HOPS:
            ref = w_ref(l, p, lax.rem(z - h + 4, 4), x)
            wait_for(ref, wr.at[l, p, h - 1])
            rcopy(ref, ref, xs.at[l, p], xr.at[l, p, h - 1], xpeer).start()

    def w_size(l, p):
        if kind(p) == PQ:
            return WQ.at[l, pl.ds(0, 80), pl.ds(0, 3 * RW)]
        if kind(p) == PA:
            return WO.at[l, pl.ds(0, 160), pl.ds(0, 3 * RW)]
        if kind(p) == PB:
            return WO.at[l, pl.ds(0, 240), pl.ds(0, 3 * RW)]
        return GU.at[l, 0, pl.ds(0, 3 * GR), :]

    @jax.named_scope("w_arrive")
    def w_arrive(l, p):
        for h in HOPS:
            wait_for(w_ref(l, p, 0, 0), xr.at[l, p, h - 1])

    def w_own(l):
        return [
            pltpu.make_async_copy(wq.at[l, sub(SH * z, SH), :], WQ.at[l, :, lane(z)], own.at[l, 0]),
            pltpu.make_async_copy(w_in.at[l, :, lan(RW + FB * z, FB)], GU.at[l, 0, sub(z * RW, RW), :], own.at[l, 1]),
            pltpu.make_async_copy(w_in.at[l, :, lan(RW + D + FB * z, FB)], GU.at[l, 1, sub(z * RW, RW), :], own.at[l, 2]),
            pltpu.make_async_copy(w_out.at[l, sub(SH * z, SH), :], WO.at[l, pl.ds(0, SH), lane(z)], own.at[l, 3]),
            pltpu.make_async_copy(w_out.at[l, sub(RW + FB * z, FB), :], WO.at[l, pl.ds(SH, FB), lane(z)], own.at[l, 4]),
        ]

    for ch in range(NE):
        gather_own(xin.at[ch], ext, ch, 0)
    for ch in range(NT):
        gather_own(xin.at[NE + ch], act, ch, NE)
    for ch in range(NE):
        ext(ch, me)[...] = xin[ch]

    def put_own(ch):
        XA[ch, rows(me)] = xin[NE + ch]
    loop(NT, put_own)
    w_send(0, "q", 0, 80)
    for l in range(2):
        for cp in w_own(l):
            cp.start()
    for hop in HOPS:
        loop(NE, lambda ch: gather_hop(ext, ch, 0, hop))

        def tokens(n):
            gather_hop(act, n, NE, hop)
            for v in range(AG0):
                w_send(0, "g", AG0 * ((hop - 1) * NT + n) + v)
        loop(NT, tokens)
    loop(NE, lambda ch: gather_cross(ext, ch, 0))
    loop(NT, lambda n: gather_cross(act, n, NE))

    @jax.named_scope("unpack")
    def unpack():
        loop(NE, lambda ch: gather_end(ext, ch, 0))

        def shard(s):
            zz, cc = s // 4, lax.rem(s, 4)
            for b in range(5):
                lo = 128 * (b // 2)
                i = 16 * (lo // CW) + s
                blk = MT[i // 5, sub(lax.rem(i, 5) * SH + 80 * (b % 2), 80), lo % CW:lo % CW + 128].astype(F32)
                for l in range(2):
                    WKV[l, sub(48 * cc, 40), lan(zz * RW + 128 * b, 128)] = blk[40 * l:40 * l + 40].astype(BF)
            i = 16 * (NE - 1) + s
            blk = MT[i // 5, rows(lax.rem(i, 5)), CW - 128:CW].astype(F32)
            for l in range(2):
                GB[l, rows(s), :] = jnp.broadcast_to(blk[:, l:l + 1], (SH, 128)).astype(BF)
        loop(16, shard)
        for l in range(2):
            for cc in range(4):
                WKV[l, 48 * cc + 40:48 * cc + 48, :] = jnp.zeros((8, D), BF)

    BR = 32

    @jax.named_scope("norm")
    def norm(l, n):
        def fold(v):
            return v.reshape(BR // 8, 8, CW).sum(0)

        def load(i):
            return XA[n, sub(i * BR, BR), :].astype(F32)

        tot = lax.fori_loop(0, D // BR, lambda i, a: a + fold(load(i)), jnp.zeros((8, CW), F32), unroll=4)
        mean = jnp.sum(tot, axis=0, keepdims=True) / D

        def square(i, a):
            d = load(i) - mean
            return a + fold(d * d)
        var = jnp.sum(lax.fori_loop(0, D // BR, square, jnp.zeros((8, CW), F32), unroll=4), axis=0, keepdims=True) / D
        scale = lax.rsqrt(var + LN_EPS)

        def put(i, a):
            g = jnp.concatenate([GB[l, sub(i * BR, BR), :].astype(F32)] * (CW // 128), axis=1)
            XA[n, sub(i * BR, BR), :] = ((load(i) - mean) * scale * g).astype(BF)
            return a
        lax.fori_loop(0, D // BR, put, 0, unroll=4)

    def tok(n):
        return lan(n * CW, CW)

    @jax.named_scope("qkv")
    def qkv(l, n):
        pos = lan(lax.rem(n * CW, SEQ), CW)
        co, si = cs[0, :, pos], cs[1, :, pos]
        h = XA[n]
        kv = jnp.dot(WKV[l], h, preferred_element_type=F32).astype(BF).astype(F32)

        def rot(lo, hi):
            return jnp.concatenate([lo * co - hi * si, hi * co + lo * si], axis=0)
        KT[:, tok(n)] = rot(kv[0:40], kv[48:88]).astype(BF)
        VT[:, tok(n)] = jnp.concatenate([kv[96:136], kv[144:184]], axis=0).astype(BF)
        qq = jnp.dot(WQ[l], h, preferred_element_type=F32).astype(BF).astype(F32)
        for hd in range(2):
            QT[HD * hd:HD * hd + HD, tok(n)] = (rot(qq[HD * hd:HD * hd + HALF], qq[HD * hd + HALF:HD * hd + HD]) * HD ** -0.5).astype(BF)

    @jax.named_scope("attention")
    def attention():
        def body(bh):
            b, hd = bh // 2, lax.rem(bh, 2)
            hr = sub(hd * HD, HD)
            for i in range(SEQ // QB):
                nk = QB * (i + 1)
                ks = lan(b * SEQ, nk)
                qs = lan(b * SEQ + QB * i, QB)
                s = dot_ta(KT[:, ks], QT[hr, qs])
                keep = lax.broadcasted_iota(jnp.int32, (QB, QB), 0) <= lax.broadcasted_iota(jnp.int32, (QB, QB), 1)
                last = jnp.where(keep, s[nk - QB:], -1e30)
                s = jnp.concatenate([s[:nk - QB], last], axis=0) if i else last
                e = jnp.exp(s - jnp.max(s, axis=0, keepdims=True))
                pr = (e * (1.0 / jnp.sum(e, axis=0, keepdims=True))).astype(BF)
                MT[b * (SEQ // CW) + QB * i // CW, hr, QB * i % CW:QB * i % CW + QB] = jnp.dot(VT[:, ks], pr, preferred_element_type=F32).astype(BF)
        loop(4, body)

    @jax.named_scope("gate_up")
    def gate_up(l, n):
        h = XA[n]
        g = dot_ta(GU[l, 0], h).astype(BF).astype(F32)
        u = dot_ta(GU[l, 1], h).astype(BF).astype(F32)
        MT[n, SH:SH + FB, :] = (g * lax.logistic(g) * u).astype(BF)

    def f(ref_value):
        return ref_value.astype(F32)

    NU = 4 * NT

    def unit(i):
        j = i // NT
        return jnp.where(j == 0, 3, jnp.where(j == 1, 0, jnp.where(j == 2, 2, 1))), lax.rem(i, NT)

    @jax.named_scope("red_a")
    def red_a(l, i):
        zz, n = unit(i)
        slot = lax.rem(i, SCN)

        @pl.when(i >= SCN)
        def _():
            wait_for(SC.at[slot], rcs.at[i - SCN])

        XA[n, sub(zz * RW, RW), :] = dot_ta(WO[l, :, lane(zz)], MT[n]).astype(BF)
        for yy in range(2):
            SC[slot, yy] = XA[n, rows(4 * zz + 2 * yy + 1 - k)]
        for yy in range(2):
            rcopy(SC.at[slot, yy], RC.at[n, 2 * zz + yy], rcs.at[i], rcr.at[i], cpeer).start()

    @jax.named_scope("red_b")
    def red_b(i):
        zz, n = unit(i)
        slot = lax.rem(i, SYN)
        wait_for(RC.at[n, pl.ds(2 * zz, 2)], rcr.at[i])

        @pl.when(i >= SYN)
        def _():
            wait_for(SY.at[slot], rys.at[i - SYN])

        SY[slot] = (f(XA[n, rows(4 * zz + 2 * (1 - y) + k)]) + f(RC[n, 2 * zz + 1 - y])).astype(BF)
        rcopy(SY.at[slot], RY.at[n, zz], rys.at[i], ryr.at[i], ypeer).start()

    def send_up(n, zz, i):
        rcopy(SZ.at[n, zz], RU.at[n, zz - 1], rsz.at[i], rzu.at[i], up).start()

    def send_down(n, zz, i):
        rcopy(SZ.at[n, zz], RD.at[n, zz], rsz.at[i], rzd.at[i], down).start()

    @jax.named_scope("red_c")
    def red_c(i):
        zz, n = unit(i)
        wait_for(RY.at[n, zz], ryr.at[i])
        SZ[n, zz] = (f(XA[n, rows(4 * zz + c)]) + f(RC[n, 2 * zz + y]) + f(RY[n, zz])).astype(BF)

        @pl.when((z == 0) & (zz > 0))
        def _():
            send_up(n, zz, i)

        @pl.when((z == 3) & (zz < 3))
        def _():
            send_down(n, zz, i)

    def relay_up(i):
        zz, n = unit(i)
        wait_for(RU.at[n, zz - 1], rzu.at[i])
        SZ[n, zz] = (f(SZ[n, zz]) + f(RU[n, zz - 1])).astype(BF)
        send_up(n, zz, i)

    def relay_down(i):
        zz, n = unit(i)
        wait_for(RD.at[n, zz], rzd.at[i])
        SZ[n, zz] = (f(SZ[n, zz]) + f(RD[n, zz])).astype(BF)
        send_down(n, zz, i)

    @jax.named_scope("red_d")
    def red_d(i):
        zz, _ = unit(i)

        @pl.when((z == 1) & (zz > 1))
        def _():
            relay_up(i)

        @pl.when((z == 2) & (zz < 2))
        def _():
            relay_down(i)

    @jax.named_scope("red_e")
    def red_e(i):
        zz, _ = unit(i)

        @pl.when((z == 2) & (zz > 2))
        def _():
            relay_up(i)

        @pl.when((z == 1) & (zz < 1))
        def _():
            relay_down(i)

    @jax.named_scope("red_f")
    def red_f(l, i):
        zz, n = unit(i)

        def finish(u):
            u = u.astype(BF)

            @pl.when(l == 0)
            def _():
                out = (f(xin[NE + n]) + f(u)).astype(BF)
                XO[n] = out
                XA[n, rows(me)] = out
                gather_own(XO.at[n], act, n, NE)

            @pl.when(l == 1)
            def _():
                yT[n] = (f(XO[n]) + f(u)).astype(BF)

        @pl.when((z == 0) & (zz == 0))
        def _():
            wait_for(RD.at[n, 0], rzd.at[i])
            finish(f(SZ[n, 0]) + f(RD[n, 0]))

        @pl.when((z == 3) & (zz == 3))
        def _():
            wait_for(RU.at[n, 2], rzu.at[i])
            finish(f(SZ[n, 3]) + f(RU[n, 2]))

        for v in (1, 2):
            @pl.when((z == v) & (zz == v))
            def _():
                wait_for(RU.at[n, v - 1], rzu.at[i])
                wait_for(RD.at[n, v], rzd.at[i])
                finish(f(SZ[n, v]) + f(RU[n, v - 1]) + f(RD[n, v]))

        @pl.when(i >= NU - SCN)
        def _():
            wait_for(SC.at[0], rcs.at[i])

        @pl.when(i >= NU - SYN)
        def _():
            wait_for(SY.at[0], rys.at[i])

        @pl.when(zz != z)
        def _():
            wait_for(SZ.at[n, zz], rsz.at[i])

    shard = me

    def o_forward(l, j):
        zz = unit(NT * j)[0]
        h = lax.rem(z - zz + 4, 4)

        @pl.when(h > 0)
        def _():
            for p in (PA, PB):
                ref = w_ref(l, p, zz, x)
                wait_for(ref, wr.at[l, p, h - 1])
                rcopy(ref, ref, xs.at[l, p], xr.at[l, p, h - 1], xpeer).start()

    def o_arrive(l, j):
        zz = unit(NT * j)[0]
        h = lax.rem(z - zz + 4, 4)

        @pl.when(h > 0)
        def _():
            for p in (PA, PB):
                wait_for(w_ref(l, p, zz, 1 - x), xr.at[l, p, h - 1])

    def layer(l):
        @pl.when(l == 0)
        def _():
            rest_send(0, 3 * NT * AG0)
            unpack()

        @pl.when(l == 1)
        def _():
            done = RS0
            for e in range(3 * NT):
                gather_hop(act, e % NT, NE, e // NT + 1)
                for v in range(AG1[e]):
                    w_send(1, "g", done)
                    done += 1
                for p in EVENTS[e]:
                    w_forward(1, p)
            loop(NT, lambda n: gather_cross(act, n, NE))
            rest_send(1, RS0 + sum(AG1))
            w_send(1, "a", 0, 160)
            w_send(1, "b", 0, 240)

        @pl.when(l == 0)
        def _():
            w_forward(0, PQ)
        for cp in w_own(l):
            cp.wait()

        def first(n):
            gather_end(act, n, NE)
            norm(l, n)
            @pl.when(n == 0)
            def _():
                w_arrive(l, PQ)
            qkv(l, n)

            late = jnp.where(l == 0, 1, LATE) + n

            @pl.when(late <= GP)
            def _():
                w_forward(l, late)
        loop(NT, first)

        @pl.when(l == 0)
        def _():
            w_send(0, "a", 0, 160)
            w_send(0, "b", 0, 240)
        attention()
        for b in range(2):
            off = lan(b * SEQ + 128 * (shard // 2), 128)
            kvo[l, 0, b] = KT[:, off]
            kvo[l, 1, b] = VT[:, off]
        fwd = jnp.where(l == 0, NT, min(GP, LATE - 1 + NT))
        loop(GP - fwd, lambda p: w_forward(l, fwd + 1 + p))
        loop(GP, lambda p: w_arrive(l, p + 1))
        o_forward(l, 0)

        def step(i):
            @pl.when(i < NU)
            def _():
                @pl.when(lax.rem(i, NT) == 0)
                def _():
                    o_arrive(l, i // NT)

                    @pl.when(i < NU - NT)
                    def _():
                        o_forward(l, i // NT + 1)

                @pl.when(i < NT)
                def _():
                    gate_up(l, i)
                red_a(l, i)
            for lag, stage in zip(LAGS, (red_b, red_c, red_d, red_e, functools.partial(red_f, l))):
                @pl.when((i >= lag) & (i < NU + lag))
                def _():
                    stage(i - lag)

            @pl.when(l == 0)
            def _():
                @pl.when(i == RQ)
                def _():
                    w_send(1, "q", 0, 80)

                @pl.when(i == RQ + 12)
                def _():
                    w_forward(1, PQ)

                base = 0
                for lo, hi, each in RG:
                    @pl.when((i >= lo) & (i < hi))
                    def _():
                        for v in range(each):
                            w_send(1, "g", base + (i - lo) * each + v)
                    base += (hi - lo) * each

                for u, ps in enumerate(UNITS):
                    if ps:
                        @pl.when(i == u)
                        def _():
                            for p in ps:
                                w_forward(1, p)
        loop(NU + LAGS[-1], step)

    loop(2, layer)

    for l in range(2):
        for p in range(NPC):
            wait_for(w_size(l, p), ws.at[l, p])
            wait_for(w_size(l, p), xs.at[l, p])


def solution(mesh):
    act_spec = P("dp", None, ("row", "col"))
    weight_spec = P(None, "row", "col")

    def device_fn(x_loc, gain_loc, w_in_loc, w_kv_loc, w_out_loc):
        me = lax.axis_index("row") * 4 + lax.axis_index("col")
        xt = x_loc.reshape(T, SH).T
        kv = jnp.transpose(w_kv_loc, (0, 2, 1)).reshape(HD, 5, 128)
        kv = jnp.concatenate([kv, jnp.zeros((HD, 1, 128), BF)], axis=1).reshape(HD, 3, 2, 128)
        kv = jnp.transpose(kv, (2, 0, 1, 3)).reshape(SH, 384)
        gain = jnp.pad(gain_loc.T, ((0, 0), (0, 126)))
        xin = jnp.concatenate([kv, gain, xt], axis=1)
        xin = jnp.transpose(xin.reshape(SH, NC, CW), (1, 0, 2))
        wq = jnp.transpose(w_in_loc[:, :, :RW], (0, 2, 1))
        NPC = GP + 3
        dma = pltpu.SemaphoreType.DMA
        hbm = pl.BlockSpec(memory_space=pl.ANY)
        vmem = pl.BlockSpec(memory_space=pltpu.VMEM)
        y_t, kvo = pl.pallas_call(
            kernel,
            out_shape=(jax.ShapeDtypeStruct((NT, SH, CW), BF), jax.ShapeDtypeStruct((2, 2, 2, HD, 128), BF)),
            in_specs=[vmem, hbm, hbm, hbm, vmem],
            out_specs=(vmem, vmem),
            scratch_shapes=[
                pltpu.VMEM((NT, D, CW), BF),
                pltpu.VMEM((2, 2, D, FB), BF),
                pltpu.VMEM((2, SH, D), BF),
                pltpu.VMEM((2, 192, D), BF),
                pltpu.VMEM((2, SH + FB, D), BF),
                pltpu.VMEM((2, D, 128), BF),
                pltpu.VMEM((NT, SH + FB, CW), BF),
                pltpu.VMEM((SH, T), BF),
                pltpu.VMEM((HD, T), BF),
                pltpu.VMEM((HD, T), BF),
                pltpu.VMEM((NT, SH, CW), BF),
                pltpu.VMEM((NT, 8, SH, CW), BF),
                pltpu.VMEM((NT, 4, SH, CW), BF),
                pltpu.VMEM((NT, 3, SH, CW), BF),
                pltpu.VMEM((NT, 3, SH, CW), BF),
                pltpu.VMEM((SCN, 2, SH, CW), BF),
                pltpu.VMEM((SYN, SH, CW), BF),
                pltpu.VMEM((NT, 4, SH, CW), BF),
                dma((NC,)), dma((NC,)), dma((NC,)), dma((NC,)),
                dma((NC, 2, 3)), dma((NC,)), dma((NC,)),
                dma((4 * NT,)), dma((4 * NT,)), dma((4 * NT,)), dma((4 * NT,)),
                dma((4 * NT,)), dma((4 * NT,)), dma((4 * NT,)),
                dma((2, NPC)), dma((2, NPC, 3)), dma((2, NPC)), dma((2, NPC, 3)),
                dma((2, 5)),
            ],
            compiler_params=pltpu.CompilerParams(collective_id=0, has_side_effects=True, vmem_limit_bytes=67043328),
        )(xin, wq, w_in_loc, w_out_loc, rope_tables())
        y = jnp.transpose(y_t, (0, 2, 1)).reshape(2, SEQ, SH)
        kv_out = lax.dynamic_slice_in_dim(kvo, 64 * lax.rem(me, 2), 64, axis=4)
        return y, jnp.transpose(kv_out, (0, 1, 2, 4, 3))

    return jax.shard_map(device_fn, mesh=mesh, in_specs=(act_spec, P(None, ("row", "col")), weight_spec, weight_spec, P(None, "col", "row")), out_specs=(act_spec, P(None, None, "dp", ("row", "col"), None)), check_vma=False)
```

time: 565 us -> 453 us (0.80); the launches traced: 558 us -> 452 us
  Pallas kernels: 546 us -> 440 us
    pallas_call x1, Pallas kernels: 546 us -> 440 us  [device_fn(): pl.pallas_call(kernel, out_shape=(jax.ShapeDtypeStruct((NT, SH, CW), BF),...]
where the time goes in v2:
time: 453 us; the launch traced here: 452 us
  Pallas kernels  440 us (97%)
  local copies, waits for them, and re-layouts  10.1 us (2%)
    pallas_call x1, Pallas kernels, device_fn(): pl.pallas_call(kernel, out_shape=(jax.ShapeDtypeStruct((NT, SH, CW), BF),...  440 us

profile of v2, /device:TPU:8, one launch (start us, length us, event | category | flops | bytes accessed | tf_op | source)
XLA Modules:
  0.0 452.5 jit_solution(10927441711875579519)
XLA Ops:
  0.7 0.6 multiply_cosine_fusion
  1.3 0.7 pad_maximum_fusion.cs
  2.1 0.0 slice-start
  2.1 1.4 slice-done
  3.5 0.0 copy-start.1
  3.5 0.0 copy-start
  3.5 2.2 copy.19
  5.7 0.0 copy-start.2
  5.7 0.0 copy-done.1
  5.7 0.1 reshape.121
  5.9 0.1 copy.11
  6.0 0.0 copy-done
  6.0 0.3 copy-done.2
  6.3 0.1 copy.12
  6.5 0.1 fusion.3
  6.6 1.0 copy.26
  7.5 440.1 %shard_map.68 = (bf16[4,160,512]{2,1,0:T(8,128)(2,1)}, bf16[2,2,2,80,128]{4,3,2,1,0:T(8,128)(2,1)}) custom-call(bf16[5,160,512]{2,1,0:T(8,128)(2,1)} %bitcast.29, bf16[2,640,640]{2,1,0:T(8,128)(2,1)} %bitcast.27, bf16[2,640,5760]{2,1,0:T(8,128)(2,1)} %w_in.1, bf16[2,3200,640]{2,1,0:T(8,128)(2,1)} %w_out.1, f32[2,40,1024]{2,1,0:T(8,128)} %pad_maximum_fusion.cs), custom_call_target="tpu_custom_call" | custom-call | tf_op jit(solution)/shard_map/pallas_call | solution.py:680
  447.7 1.0 dynamic-slice_bitcast_fusion
  448.7 0.8 copy.18
  449.5 1.6 copy.16
  451.1 0.4 reshape.126
  451.5 1.0 copy.17
  (6 shorter events, 0.1 us)
Async XLA Ops:
  2.1 1.4 slice-start
  3.5 2.2 copy-start.1
  3.5 2.5 copy-start
  5.7 0.7 copy-start.2

commit v3 on v2

--- a/solution.py
+++ b/solution.py
@@ -24,6 +24,7 @@
 NT = T // CW
 NE = 512 // CW
 NC = NE + NT
+SPC = SEQ // CW
 GP = 8
 GR = RW // GP
 LANES = 128
@@ -31,26 +32,29 @@
 QB = 256
 SCN, SYN = 4, 6
 MR = 16
-LAGS = (1, 3, 8, 12, 16)
+LAGS = (1, 4, 7, 12, 15)
 PM = GR // MR
-AG0 = 1
+S0 = (1,) * 8
+GH0, GH1 = 1, 3
+OEND = (4, 0)
+OMID = (4, 0)
+OF = (0, 4, 8)
 RQ = 0
-RG = ((1, 11, 2),)
-AG1 = (2,) * 10 + (0, 0)
-UFW, EFW = 24, 5
+SU = (0,) + (2,) * 10
+AG1 = (1,) * 8
+UFW, EFW = 30, 12
 
 
 def weight_plan():
     sent, when = 0, []
-    for lo, hi, each in RG:
-        for i in range(lo, hi):
-            when += [i] * each
-            sent += each
+    for i, each in enumerate(SU):
+        when += [i] * each
+        sent += each
     units = [[] for _ in range(4 * NT + LAGS[-1])]
     events = [[] for _ in range(3 * NT)]
     late = list(range(1, GP + 1))
     ev = []
-    for e in range(3 * NT):
+    for e in range(2 * NT):
         ev += [e] * AG1[e]
     for p in range(1, GP + 1):
         last = PM * p - 1
@@ -91,7 +95,7 @@
     return lax.dot_general(a, b, (((0,), (0,)), ((), ())), preferred_element_type=F32)
 
 
-def kernel(xin, wq, w_in, w_out, cs, yT, kvo, XA, GU, WQ, WKV, WO, GB, MT, QT, KT, VT, XO, RC, RY, RU, RD, SC, SY, SZ,
+def kernel(xin, ein, w_in, w_out, cs, yT, kvo, KVT, WT, XA, GU, WQ, WKV, WO, GB, MT, QT, KT, VT, XO, RC, RY, RU, RD, SC, SY, SZ,
            zsu, zsd, ysn, csn, zrc, yrc, crc, rcs, rcr, rys, ryr, rzu, rzd, rsz, ws, wr, xs, xr, own):
     x = lax.axis_index("dp")
     z = lax.axis_index("row")
@@ -221,7 +225,7 @@
         for h in HOPS:
             t = lax.rem(z + h, 4)
             if kind_ == "q":
-                p, src = PQ, wq.at[l, sub(SH * t + 80 * x + r, mr), :]
+                p, src = PQ, WT.at[l, sub(SH * t + 80 * x + r, mr), :]
                 dst = WQ.at[l, sub(80 * x + r, mr), lane(z)]
             elif kind_ == "g":
                 p, src = 1 + r // GR, w_in.at[l, sub(r, mr), lan(RW + D * x + FB * t, FB)]
@@ -266,37 +270,44 @@
 
     def w_own(l):
         return [
-            pltpu.make_async_copy(wq.at[l, sub(SH * z, SH), :], WQ.at[l, :, lane(z)], own.at[l, 0]),
+            None,
             pltpu.make_async_copy(w_in.at[l, :, lan(RW + FB * z, FB)], GU.at[l, 0, sub(z * RW, RW), :], own.at[l, 1]),
             pltpu.make_async_copy(w_in.at[l, :, lan(RW + D + FB * z, FB)], GU.at[l, 1, sub(z * RW, RW), :], own.at[l, 2]),
             pltpu.make_async_copy(w_out.at[l, sub(SH * z, SH), :], WO.at[l, pl.ds(0, SH), lane(z)], own.at[l, 3]),
             pltpu.make_async_copy(w_out.at[l, sub(RW + FB * z, FB), :], WO.at[l, pl.ds(SH, FB), lane(z)], own.at[l, 4]),
         ]
 
-    for ch in range(NE):
-        gather_own(xin.at[ch], ext, ch, 0)
+    def seq_part(ref, n):
+        return ref.at[n // SPC, :, lan(lax.rem(n, SPC) * CW, CW)]
+
+    q_in = [pltpu.make_async_copy(w_in.at[l, :, pl.ds(0, RW)], GU.at[1, l, sub(z * RW, RW), :], own.at[l, 5]) for l in range(2)]
+    for cp in q_in:
+        cp.start()
+    gather_own(ein, ext, 0, 0)
     for ch in range(NT):
-        gather_own(xin.at[NE + ch], act, ch, NE)
-    for ch in range(NE):
-        ext(ch, me)[...] = xin[ch]
+        gather_own(seq_part(xin, ch), act, ch, NE)
+    ext(0, me)[...] = ein[...]
 
     def put_own(ch):
-        XA[ch, rows(me)] = xin[NE + ch]
+        XA[ch, rows(me)] = seq_part(xin, ch)[...]
     loop(NT, put_own)
+    for cp in w_own(0)[1:]:
+        cp.start()
+    for l in range(2):
+        q_in[l].wait()
+        WT[l] = GU[1, l, sub(z * RW, RW), :].T
+        WQ[l, :, lane(z)] = WT[l, sub(SH * z, SH), :]
     w_send(0, "q", 0, 80)
-    for l in range(2):
-        for cp in w_own(l):
-            cp.start()
-    for hop in HOPS:
-        loop(NE, lambda ch: gather_hop(ext, ch, 0, hop))
-
-        def tokens(n):
-            gather_hop(act, n, NE, hop)
-            for v in range(AG0):
-                w_send(0, "g", AG0 * ((hop - 1) * NT + n) + v)
-        loop(NT, tokens)
-    loop(NE, lambda ch: gather_cross(ext, ch, 0))
-    loop(NT, lambda n: gather_cross(act, n, NE))
+    for cp in w_own(1)[1:]:
+        cp.start()
+    done = 0
+    for e in range(2 * NT):
+        if e % NT == 0:
+            gather_hop(ext, 0, 0, e // NT + 1)
+        gather_hop(act, e % NT, NE, e // NT + 1)
+        for v in range(S0[e]):
+            w_send(0, "g", done)
+            done += 1
 
     @jax.named_scope("unpack")
     def unpack():
@@ -363,9 +374,8 @@
             QT[HD * hd:HD * hd + HD, tok(n)] = (rot(qq[HD * hd:HD * hd + HALF], qq[HD * hd + HALF:HD * hd + HD]) * HD ** -0.5).astype(BF)
 
     @jax.named_scope("attention")
-    def attention():
-        def body(bh):
-            b, hd = bh // 2, lax.rem(bh, 2)
+    def attention(b):
+        def body(hd):
             hr = sub(hd * HD, HD)
             for i in range(SEQ // QB):
                 nk = QB * (i + 1)
@@ -378,7 +388,7 @@
                 e = jnp.exp(s - jnp.max(s, axis=0, keepdims=True))
                 pr = (e * (1.0 / jnp.sum(e, axis=0, keepdims=True))).astype(BF)
                 MT[b * (SEQ // CW) + QB * i // CW, hr, QB * i % CW:QB * i % CW + QB] = jnp.dot(VT[:, ks], pr, preferred_element_type=F32).astype(BF)
-        loop(4, body)
+        loop(2, body)
 
     @jax.named_scope("gate_up")
     def gate_up(l, n):
@@ -489,14 +499,14 @@
 
             @pl.when(l == 0)
             def _():
-                out = (f(xin[NE + n]) + f(u)).astype(BF)
+                out = (f(seq_part(xin, n)[...]) + f(u)).astype(BF)
                 XO[n] = out
                 XA[n, rows(me)] = out
                 gather_own(XO.at[n], act, n, NE)
 
             @pl.when(l == 1)
             def _():
-                yT[n] = (f(XO[n]) + f(u)).astype(BF)
+                seq_part(yT, n)[...] = (f(XO[n]) + f(u)).astype(BF)
 
         @pl.when((z == 0) & (zz == 0))
         def _():
@@ -549,36 +559,76 @@
             for p in (PA, PB):
                 wait_for(w_ref(l, p, zz, 1 - x), xr.at[l, p, h - 1])
 
+    def o_at(l, place):
+        for ll in range(2):
+            for at, cond in ((OEND[ll], (z == 0) | (z == 3)), (OMID[ll], (z == 1) | (z == 2))):
+                if isinstance(place, int):
+                    if place == at:
+                        @pl.when((l == ll) & cond)
+                        def _():
+                            o_send(l)
+                elif 0 < at <= NT:
+                    @pl.when((l == ll) & cond & (place == at))
+                    def _():
+                        o_send(l)
+
+    def o_send(l):
+        w_send(l, "a", 0, 160)
+        w_send(l, "b", 0, 240)
+
     def layer(l):
-        @pl.when(l == 0)
-        def _():
-            rest_send(0, 3 * NT * AG0)
-            unpack()
-
         @pl.when(l == 1)
         def _():
             done = RS0
-            for e in range(3 * NT):
+            for e in range(2 * NT):
                 gather_hop(act, e % NT, NE, e // NT + 1)
                 for v in range(AG1[e]):
                     w_send(1, "g", done)
                     done += 1
                 for p in EVENTS[e]:
                     w_forward(1, p)
-            loop(NT, lambda n: gather_cross(act, n, NE))
-            rest_send(1, RS0 + sum(AG1))
-            w_send(1, "a", 0, 160)
-            w_send(1, "b", 0, 240)
-
-        @pl.when(l == 0)
-        def _():
-            w_forward(0, PQ)
-        for cp in w_own(l):
-            cp.wait()
-
-        def first(n):
+
+        for ll, sent in enumerate((sum(S0), RS0 + sum(AG1))):
+            @pl.when(l == ll)
+            def _():
+                rest_send(ll, sent)
+        o_at(l, 0)
+
+        def last(n):
+            @pl.when(n < NT)
+            def _():
+                @pl.when((l == 0) & (n == 0))
+                def _():
+                    gather_hop(ext, 0, 0, len(HOPS))
+                gather_hop(act, n, NE, len(HOPS))
+                for v in range(NT):
+                    if EVENTS[2 * NT + v]:
+                        @pl.when((l == 1) & (n == v))
+                        def _():
+                            for p in EVENTS[2 * NT + v]:
+                                w_forward(1, p)
+
+                @pl.when((l == 0) & (n == 0))
+                def _():
+                    gather_cross(ext, 0, 0)
+                gather_cross(act, n, NE)
+
+            @pl.when(n > 0)
+            def _():
+                chunk(n - 1)
+
+        def chunk(n):
+            @pl.when(n == 0)
+            def _():
+                @pl.when(l == 0)
+                def _():
+                    unpack()
+                    w_forward(0, PQ)
+                for cp in w_own(l)[1:]:
+                    cp.wait()
             gather_end(act, n, NE)
             norm(l, n)
+
             @pl.when(n == 0)
             def _():
                 w_arrive(l, PQ)
@@ -589,34 +639,39 @@
             @pl.when(late <= GP)
             def _():
                 w_forward(l, late)
-        loop(NT, first)
-
-        @pl.when(l == 0)
-        def _():
-            w_send(0, "a", 0, 160)
-            w_send(0, "b", 0, 240)
-        attention()
+
+            @pl.when(lax.rem(n, SPC) == SPC - 1)
+            def _():
+                attention(n // SPC)
+            o_at(l, n + 1)
+        loop(NT + 1, last)
+        o_at(l, NT + 1)
         for b in range(2):
-            off = lan(b * SEQ + 128 * (shard // 2), 128)
-            kvo[l, 0, b] = KT[:, off]
-            kvo[l, 1, b] = VT[:, off]
+            off = lan(b * SEQ + LANES * (shard // 2), LANES)
+            for v, ref in enumerate((KT, VT)):
+                KVT[...] = ref[:, off].astype(F32).T
+                kvo[l, v, b] = KVT[sub(64 * lax.rem(shard, 2), 64), :].astype(BF)
         fwd = jnp.where(l == 0, NT, min(GP, LATE - 1 + NT))
         loop(GP - fwd, lambda p: w_forward(l, fwd + 1 + p))
+        o_at(l, NT + 2)
         loop(GP, lambda p: w_arrive(l, p + 1))
         o_forward(l, 0)
+        gh = jnp.where(l == 0, GH0, GH1)
+        loop(gh, lambda n: gate_up(l, n))
 
         def step(i):
             @pl.when(i < NU)
             def _():
+                for j, u in enumerate(OF):
+                    @pl.when(i == u)
+                    def _():
+                        o_forward(l, j + 1)
+
                 @pl.when(lax.rem(i, NT) == 0)
                 def _():
                     o_arrive(l, i // NT)
 
-                    @pl.when(i < NU - NT)
-                    def _():
-                        o_forward(l, i // NT + 1)
-
-                @pl.when(i < NT)
+                @pl.when((i >= gh) & (i < NT))
                 def _():
                     gate_up(l, i)
                 red_a(l, i)
@@ -635,13 +690,11 @@
                 def _():
                     w_forward(1, PQ)
 
-                base = 0
-                for lo, hi, each in RG:
-                    @pl.when((i >= lo) & (i < hi))
-                    def _():
-                        for v in range(each):
-                            w_send(1, "g", base + (i - lo) * each + v)
-                    base += (hi - lo) * each
+                for u, each in enumerate(SU):
+                    if each:
+                        @pl.when(i == u)
+                        def _():
+                            loop(each, lambda v: w_send(1, "g", sum(SU[:u]) + v))
 
                 for u, ps in enumerate(UNITS):
                     if ps:
@@ -664,25 +717,22 @@
     weight_spec = P(None, "row", "col")
 
     def device_fn(x_loc, gain_loc, w_in_loc, w_kv_loc, w_out_loc):
-        me = lax.axis_index("row") * 4 + lax.axis_index("col")
-        xt = x_loc.reshape(T, SH).T
-        kv = jnp.transpose(w_kv_loc, (0, 2, 1)).reshape(HD, 5, 128)
-        kv = jnp.concatenate([kv, jnp.zeros((HD, 1, 128), BF)], axis=1).reshape(HD, 3, 2, 128)
-        kv = jnp.transpose(kv, (2, 0, 1, 3)).reshape(SH, 384)
-        gain = jnp.pad(gain_loc.T, ((0, 0), (0, 126)))
-        xin = jnp.concatenate([kv, gain, xt], axis=1)
-        xin = jnp.transpose(xin.reshape(SH, NC, CW), (1, 0, 2))
-        wq = jnp.transpose(w_in_loc[:, :, :RW], (0, 2, 1))
+        kv = jnp.transpose(w_kv_loc, (0, 2, 1)).reshape(HD, RW)
+        kv = jnp.concatenate([jnp.concatenate([kv[:, v:v + LANES], kv[:, v + LANES:v + 2 * LANES]], axis=0) for v in (0, 2 * LANES)] + [jnp.pad(kv[:, 4 * LANES:], ((0, SH - HD), (0, 0)))], axis=1)
+        gain = jnp.pad(gain_loc.T, ((0, 0), (0, LANES - 2)))
+        ein = jnp.concatenate([kv, gain], axis=1)
         NPC = GP + 3
         dma = pltpu.SemaphoreType.DMA
         hbm = pl.BlockSpec(memory_space=pl.ANY)
         vmem = pl.BlockSpec(memory_space=pltpu.VMEM)
         y_t, kvo = pl.pallas_call(
             kernel,
-            out_shape=(jax.ShapeDtypeStruct((NT, SH, CW), BF), jax.ShapeDtypeStruct((2, 2, 2, HD, 128), BF)),
-            in_specs=[vmem, hbm, hbm, hbm, vmem],
+            out_shape=(jax.ShapeDtypeStruct((2, SH, SEQ), BF), jax.ShapeDtypeStruct((2, 2, 2, SEQ // 16, HD), BF)),
+            in_specs=[vmem, vmem, hbm, hbm, vmem],
             out_specs=(vmem, vmem),
             scratch_shapes=[
+                pltpu.VMEM((LANES, HD), F32),
+                pltpu.VMEM((2, RW, RW), BF),
                 pltpu.VMEM((NT, D, CW), BF),
                 pltpu.VMEM((2, 2, D, FB), BF),
                 pltpu.VMEM((2, SH, D), BF),
@@ -706,12 +756,10 @@
                 dma((4 * NT,)), dma((4 * NT,)), dma((4 * NT,)), dma((4 * NT,)),
                 dma((4 * NT,)), dma((4 * NT,)), dma((4 * NT,)),
                 dma((2, NPC)), dma((2, NPC, 3)), dma((2, NPC)), dma((2, NPC, 3)),
-                dma((2, 5)),
+                dma((2, 6)),
             ],
             compiler_params=pltpu.CompilerParams(collective_id=0, has_side_effects=True, vmem_limit_bytes=67043328),
-        )(xin, wq, w_in_loc, w_out_loc, rope_tables())
-        y = jnp.transpose(y_t, (0, 2, 1)).reshape(2, SEQ, SH)
-        kv_out = lax.dynamic_slice_in_dim(kvo, 64 * lax.rem(me, 2), 64, axis=4)
-        return y, jnp.transpose(kv_out, (0, 1, 2, 4, 3))
+        )(jnp.transpose(x_loc, (0, 2, 1)), ein, w_in_loc, w_out_loc, rope_tables())
+        return jnp.transpose(y_t, (0, 2, 1)), kvo
 
     return jax.shard_map(device_fn, mesh=mesh, in_specs=(act_spec, P(None, ("row", "col")), weight_spec, weight_spec, P(None, "col", "row")), out_specs=(act_spec, P(None, None, "dp", ("row", "col"), None)), check_vma=False)

time: 453 us -> 441 us (0.974)
  Pallas kernels: 440 us -> 433 us
  local copies, waits for them, and re-layouts: 10.1 us -> 5.16 us
    pallas_call x1, Pallas kernels: 440 us -> 433 us  [device_fn(): pl.pallas_call(kernel, out_shape=(jax.ShapeDtypeStruct((2, SH, SEQ), BF),...]
where the time goes in v3:
time: 441 us
  Pallas kernels  433 us (98%)
  local copies, waits for them, and re-layouts  5.16 us (1%)
    pallas_call x1, Pallas kernels, device_fn(): pl.pallas_call(kernel, out_shape=(jax.ShapeDtypeStruct((2, SH, SEQ), BF),...  433 us

profile of v3, /device:TPU:8, one launch (start us, length us, event | category | flops | bytes accessed | tf_op | source)
XLA Modules:
  0.0 441.1 jit_solution(10713333054493193894)
XLA Ops:
  0.7 0.8 copy.7
  1.5 0.8 fusion.5
  2.3 0.7 fusion.4.ein
  3.0 0.6 multiply_cosine_fusion
  3.6 0.7 pad_maximum_fusion.cs
  4.4 433.2 %shard_map.68 = (bf16[2,160,1024]{2,1,0:T(8,128)(2,1)}, bf16[2,2,2,64,80]{4,3,2,1,0:T(8,128)(2,1)}) custom-call(bf16[2,160,1024]{2,1,0:T(8,128)(2,1)} %bitcast.6, bf16[160,512]{1,0:T(8,128)(2,1)} %fusion.4.ein, bf16[2,640,5760]{2,1,0:T(8,128)(2,1)} %w_in.1, bf16[2,3200,640]{2,1,0:T(8,128)(2,1)} %w_out.1, f32[2,40,1024]{2,1,0:T(8,128)} %pad_maximum_fusion.cs), custom_call_target="tpu_custom_call" | custom-call | tf_op jit(solution)/shard_map/pallas_call | solution.py:728
  437.6 2.0 copy.10
  439.6 1.6 copy.11
  (2 shorter events, 0.0 us)

commit v4 on v3

--- a/solution.py
+++ b/solution.py
@@ -37,11 +37,11 @@
 S0 = (1,) * 8
 GH0, GH1 = 1, 3
 OEND = (4, 0)
-OMID = (4, 0)
+OMID = (5, 5)
 OF = (0, 4, 8)
 RQ = 0
 SU = (0,) + (2,) * 10
-AG1 = (1,) * 8
+AG1 = (0,) * 8
 UFW, EFW = 30, 12
 
 

time: 441 us -> 435 us (0.986)
  Pallas kernels: 433 us -> 427 us
    pallas_call x1, Pallas kernels: 433 us -> 427 us  [device_fn(): pl.pallas_call(kernel, out_shape=(jax.ShapeDtypeStruct((2, SH, SEQ), BF),...]
where the time goes in v4:
time: 435 us
  Pallas kernels  427 us (98%)
  local copies, waits for them, and re-layouts  5.16 us (1%)
    pallas_call x1, Pallas kernels, device_fn(): pl.pallas_call(kernel, out_shape=(jax.ShapeDtypeStruct((2, SH, SEQ), BF),...  427 us

profile of v4, /device:TPU:8, one launch (start us, length us, event | category | flops | bytes accessed | tf_op | source)
XLA Modules:
  0.0 434.9 jit_solution(3408112908539211540)
XLA Ops:
  0.7 0.8 copy.7
  1.5 0.8 fusion.5
  2.3 0.7 fusion.4.ein
  3.0 0.6 multiply_cosine_fusion
  3.6 0.7 pad_maximum_fusion.cs
  4.4 427.0 %shard_map.68 = (bf16[2,160,1024]{2,1,0:T(8,128)(2,1)}, bf16[2,2,2,64,80]{4,3,2,1,0:T(8,128)(2,1)}) custom-call(bf16[2,160,1024]{2,1,0:T(8,128)(2,1)} %bitcast.6, bf16[160,512]{1,0:T(8,128)(2,1)} %fusion.4.ein, bf16[2,640,5760]{2,1,0:T(8,128)(2,1)} %w_in.1, bf16[2,3200,640]{2,1,0:T(8,128)(2,1)} %w_out.1, f32[2,40,1024]{2,1,0:T(8,128)} %pad_maximum_fusion.cs), custom_call_target="tpu_custom_call" | custom-call | tf_op jit(solution)/shard_map/pallas_call | solution.py:728
  431.4 2.0 copy.10
  433.3 1.6 copy.11
  (2 shorter events, 0.0 us)

commit v5 on v4

--- a/solution.py
+++ b/solution.py
@@ -28,6 +28,7 @@
 GP = 8
 GR = RW // GP
 LANES = 128
+EW = 3 * LANES
 HOPS = (1, 2, 3)
 QB = 256
 SCN, SYN = 4, 6
@@ -80,7 +81,7 @@
 def rope_tables():
     inv_freq = 1.0 / (10000.0 ** (jnp.arange(HALF, dtype=F32) * 2.0 / HD))
     angles = inv_freq[:, None] * jnp.arange(SEQ).astype(F32)[None, :]
-    return jnp.stack([jnp.cos(angles), jnp.sin(angles)])
+    return jnp.cos(angles), jnp.sin(angles)
 
 
 def sub(start, size):
@@ -95,7 +96,7 @@
     return lax.dot_general(a, b, (((0,), (0,)), ((), ())), preferred_element_type=F32)
 
 
-def kernel(xin, ein, w_in, w_out, cs, yT, kvo, KVT, WT, XA, GU, WQ, WKV, WO, GB, MT, QT, KT, VT, XO, RC, RY, RU, RD, SC, SY, SZ,
+def kernel(xin, kvw, gn, w_in, w_out, cos, sin, yT, kvo, EIN, KVT, WT, XA, GU, WQ, WKV, WO, GB, MT, QT, KT, VT, XO, RC, RY, RU, RD, SC, SY, SZ,
            zsu, zsd, ysn, csn, zrc, yrc, crc, rcs, rcr, rys, ryr, rzu, rzd, rsz, ws, wr, xs, xr, own):
     x = lax.axis_index("dp")
     z = lax.axis_index("row")
@@ -134,7 +135,11 @@
 
     def ext(ch, s):
         i = 16 * ch + s
-        return MT.at[i // 5, rows(lax.rem(i, 5))]
+        return MT.at[i // 5, rows(lax.rem(i, 5)), pl.ds(0, EW)]
+
+    @jax.named_scope("gather_own")
+    def size(o, shards):
+        return XA.at[0, pl.ds(0, shards * SH), pl.ds(0, CW if o else EW)]
 
     @jax.named_scope("gather_own")
     def gather_own(src, buf, ch, o):
@@ -181,7 +186,7 @@
     @jax.named_scope("gather_cross")
     def gather_cross(buf, ch, o):
         q = ch + o
-        wait_for(XA.at[0, pl.ds(0, 4 * SH)], yrc.at[q])
+        wait_for(size(o, 4), yrc.at[q])
         for zz in range(4):
             ref = buf(ch, 4 * zz + lax.rem(c + 2, 4))
             rcopy(ref, ref, csn.at[q], crc.at[q], cpeer).start()
@@ -189,17 +194,17 @@
     @jax.named_scope("gather_end")
     def gather_end(buf, ch, o):
         q = ch + o
-        wait_for(XA.at[0, pl.ds(0, 8 * SH)], crc.at[q])
+        wait_for(size(o, 8), crc.at[q])
         for zz in range(3):
             @pl.when(z == zz)
             def _():
-                wait_for(XA.at[0, pl.ds(0, (zz + 1) * SH)], zsu.at[q])
+                wait_for(size(o, zz + 1), zsu.at[q])
 
             @pl.when(z == 3 - zz)
             def _():
-                wait_for(XA.at[0, pl.ds(0, (zz + 1) * SH)], zsd.at[q])
-        wait_for(XA.at[0, pl.ds(0, 4 * SH)], ysn.at[q])
-        wait_for(XA.at[0, pl.ds(0, 8 * SH)], csn.at[q])
+                wait_for(size(o, zz + 1), zsd.at[q])
+        wait_for(size(o, 4), ysn.at[q])
+        wait_for(size(o, 8), csn.at[q])
 
     NPC = GP + 3
 
@@ -283,14 +288,18 @@
     q_in = [pltpu.make_async_copy(w_in.at[l, :, pl.ds(0, RW)], GU.at[1, l, sub(z * RW, RW), :], own.at[l, 5]) for l in range(2)]
     for cp in q_in:
         cp.start()
-    gather_own(ein, ext, 0, 0)
-    for ch in range(NT):
-        gather_own(seq_part(xin, ch), act, ch, NE)
-    ext(0, me)[...] = ein[...]
+    for b in range(5):
+        blk = jnp.concatenate([kvw[l, :, LANES * b:LANES * (b + 1)].astype(F32) for l in range(2)], axis=0)
+        EIN[HD * (b % 2):HD * (b % 2) + HD, LANES * (b // 2):LANES * (b // 2 + 1)] = blk.astype(BF)
+    EIN[HD:, 2 * LANES:] = gn[...]
+    ext(0, me)[...] = EIN[...]
 
     def put_own(ch):
         XA[ch, rows(me)] = seq_part(xin, ch)[...]
     loop(NT, put_own)
+    gather_own(EIN, ext, 0, 0)
+    for ch in range(NT):
+        gather_own(seq_part(xin, ch), act, ch, NE)
     for cp in w_own(0)[1:]:
         cp.start()
     for l in range(2):
@@ -321,10 +330,10 @@
                 blk = MT[i // 5, sub(lax.rem(i, 5) * SH + 80 * (b % 2), 80), lo % CW:lo % CW + 128].astype(F32)
                 for l in range(2):
                     WKV[l, sub(48 * cc, 40), lan(zz * RW + 128 * b, 128)] = blk[40 * l:40 * l + 40].astype(BF)
-            i = 16 * (NE - 1) + s
-            blk = MT[i // 5, rows(lax.rem(i, 5)), CW - 128:CW].astype(F32)
+            blk = MT[s // 5, sub(lax.rem(s, 5) * SH + HD, HD), 2 * LANES:EW].astype(F32)
             for l in range(2):
-                GB[l, rows(s), :] = jnp.broadcast_to(blk[:, l:l + 1], (SH, 128)).astype(BF)
+                for v in range(2):
+                    GB[l, sub(s * SH + HD * v, HD), :] = jnp.broadcast_to(blk[:, l + 2 * v:l + 2 * v + 1], (HD, LANES)).astype(BF)
         loop(16, shard)
         for l in range(2):
             for cc in range(4):
@@ -361,7 +370,7 @@
     @jax.named_scope("qkv")
     def qkv(l, n):
         pos = lan(lax.rem(n * CW, SEQ), CW)
-        co, si = cs[0, :, pos], cs[1, :, pos]
+        co, si = cos[:, pos], sin[:, pos]
         h = XA[n]
         kv = jnp.dot(WKV[l], h, preferred_element_type=F32).astype(BF).astype(F32)
 
@@ -717,10 +726,7 @@
     weight_spec = P(None, "row", "col")
 
     def device_fn(x_loc, gain_loc, w_in_loc, w_kv_loc, w_out_loc):
-        kv = jnp.transpose(w_kv_loc, (0, 2, 1)).reshape(HD, RW)
-        kv = jnp.concatenate([jnp.concatenate([kv[:, v:v + LANES], kv[:, v + LANES:v + 2 * LANES]], axis=0) for v in (0, 2 * LANES)] + [jnp.pad(kv[:, 4 * LANES:], ((0, SH - HD), (0, 0)))], axis=1)
-        gain = jnp.pad(gain_loc.T, ((0, 0), (0, LANES - 2)))
-        ein = jnp.concatenate([kv, gain], axis=1)
+        gain = jnp.pad(jnp.transpose(gain_loc.reshape(2, 2, HD), (2, 1, 0)).reshape(HD, 4), ((0, 0), (0, LANES - 4)))
         NPC = GP + 3
         dma = pltpu.SemaphoreType.DMA
         hbm = pl.BlockSpec(memory_space=pl.ANY)
@@ -728,9 +734,10 @@
         y_t, kvo = pl.pallas_call(
             kernel,
             out_shape=(jax.ShapeDtypeStruct((2, SH, SEQ), BF), jax.ShapeDtypeStruct((2, 2, 2, SEQ // 16, HD), BF)),
-            in_specs=[vmem, vmem, hbm, hbm, vmem],
+            in_specs=[vmem, vmem, vmem, hbm, hbm, vmem, vmem],
             out_specs=(vmem, vmem),
             scratch_shapes=[
+                pltpu.VMEM((SH, EW), BF),
                 pltpu.VMEM((LANES, HD), F32),
                 pltpu.VMEM((2, RW, RW), BF),
                 pltpu.VMEM((NT, D, CW), BF),
@@ -759,7 +766,7 @@
                 dma((2, 6)),
             ],
             compiler_params=pltpu.CompilerParams(collective_id=0, has_side_effects=True, vmem_limit_bytes=67043328),
-        )(jnp.transpose(x_loc, (0, 2, 1)), ein, w_in_loc, w_out_loc, rope_tables())
+        )(jnp.transpose(x_loc, (0, 2, 1)), jnp.transpose(w_kv_loc, (0, 2, 1)), gain, w_in_loc, w_out_loc, *rope_tables())
         return jnp.transpose(y_t, (0, 2, 1)), kvo
 
     return jax.shard_map(device_fn, mesh=mesh, in_specs=(act_spec, P(None, ("row", "col")), weight_spec, weight_spec, P(None, "col", "row")), out_specs=(act_spec, P(None, None, "dp", ("row", "col"), None)), check_vma=False)

time: 435 us -> 433 us (level)
  no operation moved by 1% of the time
where the time goes in v5:
time: 433 us
  Pallas kernels  426 us (98%)
  local copies, waits for them, and re-layouts  5.04 us (1%)
    pallas_call x1, Pallas kernels, device_fn(): pl.pallas_call(kernel, out_shape=(jax.ShapeDtypeStruct((2, SH, SEQ), BF),...  426 us

profile of v5, /device:TPU:8, one launch (start us, length us, event | category | flops | bytes accessed | tf_op | source)
XLA Modules:
  0.0 432.8 jit_solution(6519127433310397757)
XLA Ops:
  0.6 0.8 reshape.20
  1.4 0.1 copy.9
  1.5 0.6 pad.4.gn
  2.2 1.4 multiply_sine_fusion
  3.5 425.7 %shard_map.68 = (bf16[2,160,1024]{2,1,0:T(8,128)(2,1)}, bf16[2,2,2,64,80]{4,3,2,1,0:T(8,128)(2,1)}) custom-call(bf16[2,160,1024]{2,1,0:T(8,128)(2,1)} %bitcast.6, bf16[2,40,640]{2,1,0:T(8,128)(2,1)} %bitcast.8, bf16[80,128]{1,0:T(8,128)(2,1)} %pad.4.gn, bf16[2,640,5760]{2,1,0:T(8,128)(2,1)} %w_in.1, bf16[2,3200,640]{2,1,0:T(8,128)(2,1)} %w_out.1, ...), custom_call_target="tpu_custom_call" | custom-call | tf_op jit(solution)/shard_map/pallas_call | solution.py:734
  429.2 2.0 copy.12
  431.2 1.6 copy.13
  (3 shorter events, 0.0 us)

commit v6 on v5

--- a/solution.py
+++ b/solution.py
@@ -1,5 +1,3 @@
-import functools
-
 import jax
 import jax.numpy as jnp
 from jax import lax
@@ -33,16 +31,16 @@
 QB = 256
 SCN, SYN = 4, 6
 MR = 16
-LAGS = (1, 4, 7, 12, 15)
+LAGS = (1, 6, 12, 4, 18)
 PM = GR // MR
-S0 = (1,) * 8
+S0 = (0,) * 4 + (2,) * 4
 GH0, GH1 = 1, 3
 OEND = (4, 0)
 OMID = (5, 5)
 OF = (0, 4, 8)
 RQ = 0
 SU = (0,) + (2,) * 10
-AG1 = (0,) * 8
+AG1 = (0,) * len(S0)
 UFW, EFW = 30, 12
 
 
@@ -250,8 +248,6 @@
         for v in range(whole, GP):
             w_send(l, "g", v, GR)
 
-    NQ, NG, NA, NB = 80 // MR, RW // MR, 160 // MR, 240 // MR
-
     @jax.named_scope("w_forward")
     def w_forward(l, p):
         for h in HOPS:
@@ -431,7 +427,7 @@
             rcopy(SC.at[slot, yy], RC.at[n, 2 * zz + yy], rcs.at[i], rcr.at[i], cpeer).start()
 
     @jax.named_scope("red_b")
-    def red_b(i):
+    def red_b(l, i):
         zz, n = unit(i)
         slot = lax.rem(i, SYN)
         wait_for(RC.at[n, pl.ds(2 * zz, 2)], rcr.at[i])
@@ -450,7 +446,7 @@
         rcopy(SZ.at[n, zz], RD.at[n, zz], rsz.at[i], rzd.at[i], down).start()
 
     @jax.named_scope("red_c")
-    def red_c(i):
+    def red_c(l, i):
         zz, n = unit(i)
         wait_for(RY.at[n, zz], ryr.at[i])
         SZ[n, zz] = (f(XA[n, rows(4 * zz + c)]) + f(RC[n, 2 * zz + y]) + f(RY[n, zz])).astype(BF)
@@ -476,7 +472,7 @@
         send_down(n, zz, i)
 
     @jax.named_scope("red_d")
-    def red_d(i):
+    def red_d(l, i):
         zz, _ = unit(i)
 
         @pl.when((z == 1) & (zz > 1))
@@ -488,7 +484,7 @@
             relay_down(i)
 
     @jax.named_scope("red_e")
-    def red_e(i):
+    def red_e(l, i):
         zz, _ = unit(i)
 
         @pl.when((z == 2) & (zz > 2))
@@ -668,26 +664,27 @@
         gh = jnp.where(l == 0, GH0, GH1)
         loop(gh, lambda n: gate_up(l, n))
 
+        def head(l, i):
+            for j, u in enumerate(OF):
+                @pl.when(i == u)
+                def _():
+                    o_forward(l, j + 1)
+
+            @pl.when(lax.rem(i, NT) == 0)
+            def _():
+                o_arrive(l, i // NT)
+
+            @pl.when((i >= gh) & (i < NT))
+            def _():
+                gate_up(l, i)
+            red_a(l, i)
+
+
         def step(i):
-            @pl.when(i < NU)
-            def _():
-                for j, u in enumerate(OF):
-                    @pl.when(i == u)
-                    def _():
-                        o_forward(l, j + 1)
-
-                @pl.when(lax.rem(i, NT) == 0)
-                def _():
-                    o_arrive(l, i // NT)
-
-                @pl.when((i >= gh) & (i < NT))
-                def _():
-                    gate_up(l, i)
-                red_a(l, i)
-            for lag, stage in zip(LAGS, (red_b, red_c, red_d, red_e, functools.partial(red_f, l))):
+            for lag, stage in zip((0, *LAGS), (head, red_b, red_d, red_e, red_c, red_f)):
                 @pl.when((i >= lag) & (i < NU + lag))
                 def _():
-                    stage(i - lag)
+                    stage(l, i - lag)
 
             @pl.when(l == 0)
             def _():

time: 433 us -> 425 us (0.982)
  Pallas kernels: 426 us -> 417 us
    pallas_call x1, Pallas kernels: 426 us -> 417 us  [device_fn(): pl.pallas_call(kernel, out_shape=(jax.ShapeDtypeStruct((2, SH, SEQ), BF),...]
where the time goes in v6:
time: 425 us
  Pallas kernels  417 us (98%)
  local copies, waits for them, and re-layouts  5.04 us (1%)
    pallas_call x1, Pallas kernels, device_fn(): pl.pallas_call(kernel, out_shape=(jax.ShapeDtypeStruct((2, SH, SEQ), BF),...  417 us

profile of v6, /device:TPU:8, one launch (start us, length us, event | category | flops | bytes accessed | tf_op | source)
XLA Modules:
  0.0 424.5 jit_solution(16212115916905341844)
XLA Ops:
  0.6 0.8 reshape.20
  1.4 0.1 copy.9
  1.5 0.6 pad.4.gn
  2.2 1.4 multiply_sine_fusion
  3.5 417.5 %shard_map.68 = (bf16[2,160,1024]{2,1,0:T(8,128)(2,1)}, bf16[2,2,2,64,80]{4,3,2,1,0:T(8,128)(2,1)}) custom-call(bf16[2,160,1024]{2,1,0:T(8,128)(2,1)} %bitcast.6, bf16[2,40,640]{2,1,0:T(8,128)(2,1)} %bitcast.8, bf16[80,128]{1,0:T(8,128)(2,1)} %pad.4.gn, bf16[2,640,5760]{2,1,0:T(8,128)(2,1)} %w_in.1, bf16[2,3200,640]{2,1,0:T(8,128)(2,1)} %w_out.1, ...), custom_call_target="tpu_custom_call" | custom-call | tf_op jit(solution)/shard_map/pallas_call | solution.py:731
  421.0 2.0 copy.12
  423.0 1.6 copy.13
  (3 shorter events, 0.0 us)

commit v7 on v6

--- a/solution.py
+++ b/solution.py
@@ -38,7 +38,7 @@
 OEND = (4, 0)
 OMID = (5, 5)
 OF = (0, 4, 8)
-RQ = 0
+RQ = 1
 SU = (0,) + (2,) * 10
 AG1 = (0,) * len(S0)
 UFW, EFW = 30, 12

time: 425 us -> 425 us (level)
  no operation moved by 1% of the time
where the time goes in v7:
time: 425 us; the launch traced here: 424 us
  Pallas kernels  417 us (98%)
  local copies, waits for them, and re-layouts  5.04 us (1%)
    pallas_call x1, Pallas kernels, device_fn(): pl.pallas_call(kernel, out_shape=(jax.ShapeDtypeStruct((2, SH, SEQ), BF),...  417 us

profile of v7, /device:TPU:8, one launch (start us, length us, event | category | flops | bytes accessed | tf_op | source)
XLA Modules:
  0.0 423.8 jit_solution(13149068720402893022)
XLA Ops:
  0.6 0.8 reshape.20
  1.4 0.1 copy.9
  1.5 0.6 pad.4.gn
  2.2 1.4 multiply_sine_fusion
  3.5 416.7 %shard_map.68 = (bf16[2,160,1024]{2,1,0:T(8,128)(2,1)}, bf16[2,2,2,64,80]{4,3,2,1,0:T(8,128)(2,1)}) custom-call(bf16[2,160,1024]{2,1,0:T(8,128)(2,1)} %bitcast.6, bf16[2,40,640]{2,1,0:T(8,128)(2,1)} %bitcast.8, bf16[80,128]{1,0:T(8,128)(2,1)} %pad.4.gn, bf16[2,640,5760]{2,1,0:T(8,128)(2,1)} %w_in.1, bf16[2,3200,640]{2,1,0:T(8,128)(2,1)} %w_out.1, ...), custom_call_target="tpu_custom_call" | custom-call | tf_op jit(solution)/shard_map/pallas_call | solution.py:731
  420.2 2.0 copy.12
  422.2 1.6 copy.13
  (3 shorter events, 0.0 us)
